TPU v7x, 16 devices: a 4x2x1 block of a 4x4x8 slice. The times are simulated.
16 devices in a mesh: dp: 2 (over y, z), ep: 8 (over x, core).
Axes of the slice: x: 4, y: 2, z: 1, core: 2. Of those that a mesh axis runs over, the one named last changes fastest.
The devices are a block of a 4x4x8 slice.
Arguments:
- x_tokens: bfloat16 [1024, 1536], P(('dp', 'ep')), parts along dimension 0
- dy_tokens: bfloat16 [1024, 1536], P(('dp', 'ep')), parts along dimension 0
- expert_ids: int32 [1024, 8], P(('dp', 'ep')), parts along dimension 0
- gate_vals: float32 [1024, 8], P(('dp', 'ep')), parts along dimension 0
- slot_ids: int32 [1024, 8], P(('dp', 'ep')), parts along dimension 0
- w_gate: bfloat16 [40, 1536, 512], P('ep')
- w_down: bfloat16 [40, 512, 1536], P('ep')
- w_up: bfloat16 [40, 1536, 512], P('ep')
Outputs:
- output 1: bfloat16 [1024, 1536], P(('dp', 'ep')), parts along dimension 0
- output 2: float32 [80, 1536, 512], P(('dp', 'ep')), parts along dimension 0
- output 3: float32 [80, 512, 1536], P(('dp', 'ep')), parts along dimension 0
- output 4: float32 [80, 1536, 512], P(('dp', 'ep')), parts along dimension 0
There are 2 independent parts. A program takes and returns all parts, laid end to end along the dimension named above; an argument that names none is the same for every part.
All inputs are finite; a program needn't handle non-finite values.
Results may differ from a plain program's by a relative error of at most 0.0103792.
Values are sent between devices in bfloat16 or wider.
A program may use at most 768 MiB of HBM per device.

v0:
```python
import jax
import jax.numpy as jnp
from jax import lax
from jax.sharding import PartitionSpec as P


def slot_capacity(tok_dev, top_k, n_exp):
    return ((3 * tok_dev * top_k) // (2 * n_exp) + 7) // 8 * 8


def source_dispatch(x_src, dy_src, ids_src, gate_src, slot_src, cap_rows, n_exp):
    tok_dev, top_k = ids_src.shape
    n_copy = tok_dev * top_k
    d_model = x_src.shape[1]
    flat_slot = jnp.where(slot_src >= 0, ids_src * cap_rows + slot_src, n_exp * cap_rows)
    slot_copy = jnp.full((n_exp * cap_rows,), n_copy, jnp.int32).at[flat_slot.reshape(n_copy)].set(jnp.arange(n_copy, dtype=jnp.int32), mode='drop')
    slot_tok = slot_copy // top_k
    x_send = jnp.take(x_src, slot_tok, axis=0, mode='fill', fill_value=0)
    dy_send = jnp.take(dy_src, slot_tok, axis=0, mode='fill', fill_value=0)
    gate_slot = jnp.take(gate_src.reshape(n_copy), slot_copy, mode='fill', fill_value=0)
    dz_send = (gate_slot[:, None] * dy_send).astype(jnp.bfloat16)
    return x_send.reshape(n_exp, cap_rows, d_model), dz_send.reshape(n_exp, cap_rows, d_model), flat_slot


def source_combine(dx_send, flat_slot):
    n_exp, cap_rows, d_model = dx_send.shape
    rows = jnp.take(dx_send.reshape(n_exp * cap_rows, d_model), flat_slot, axis=0, mode='fill', fill_value=0)
    return jnp.sum(rows, axis=1, dtype=jnp.float32).astype(jnp.bfloat16)


def expert_backward(x_rows, dz_rows, w_gate, w_down, w_up):
    a_pre = jnp.einsum('erd,edf->erf', x_rows, w_gate, preferred_element_type=jnp.float32).astype(jnp.bfloat16).astype(jnp.float32)
    b_pre = jnp.einsum('erd,edf->erf', x_rows, w_up, preferred_element_type=jnp.float32).astype(jnp.bfloat16).astype(jnp.float32)
    sigma_a = jax.nn.sigmoid(a_pre)
    silu_a = a_pre * sigma_a
    hidden = (silu_a * b_pre).astype(jnp.bfloat16)
    d_hidden = jnp.einsum('erd,efd->erf', dz_rows, w_down, preferred_element_type=jnp.float32)
    d_gate = (d_hidden * b_pre * sigma_a * (1.0 + a_pre * (1.0 - sigma_a))).astype(jnp.bfloat16)
    d_up = (d_hidden * silu_a).astype(jnp.bfloat16)
    g_down = jnp.einsum('erf,erd->efd', hidden, dz_rows, preferred_element_type=jnp.float32)
    g_gate = jnp.einsum('erd,erf->edf', x_rows, d_gate, preferred_element_type=jnp.float32)
    g_up = jnp.einsum('erd,erf->edf', x_rows, d_up, preferred_element_type=jnp.float32)
    dx_rows = (jnp.einsum('erf,edf->erd', d_gate, w_gate, preferred_element_type=jnp.float32) + jnp.einsum('erf,edf->erd', d_up, w_up, preferred_element_type=jnp.float32)).astype(jnp.bfloat16)
    return dx_rows, g_gate, g_down, g_up


def solution(mesh):
    n_dev = mesh.shape['ep']

    def local_step(x_loc, dy_loc, ids_loc, gate_loc, slot_loc, w_gate, w_down, w_up):
        tok_dev, top_k = ids_loc.shape
        n_local = w_gate.shape[0]
        n_exp = n_local * n_dev
        d_model = x_loc.shape[1]
        cap_rows = slot_capacity(tok_dev, top_k, n_exp)
        x_send, dz_send, flat_slot = source_dispatch(x_loc, dy_loc, ids_loc, gate_loc, slot_loc, cap_rows, n_exp)
        x_recv = lax.all_to_all(x_send.reshape(n_exp, 1, cap_rows, d_model), 'ep', 0, 1, tiled=True)
        dz_recv = lax.all_to_all(dz_send.reshape(n_exp, 1, cap_rows, d_model), 'ep', 0, 1, tiled=True)
        dx_rows, g_gate, g_down, g_up = expert_backward(x_recv.reshape(n_local, n_dev * cap_rows, d_model), dz_recv.reshape(n_local, n_dev * cap_rows, d_model), w_gate, w_down, w_up)
        dx_back = lax.all_to_all(dx_rows.reshape(n_local, n_dev, cap_rows, d_model), 'ep', 1, 0, tiled=True)
        dx_loc = source_combine(dx_back.reshape(n_exp, cap_rows, d_model), flat_slot)
        return dx_loc, g_gate, g_down, g_up

    tok_spec = P(('dp', 'ep'), None)
    w_spec = P('ep', None, None)
    grad_spec = P(('dp', 'ep'), None, None)
    return jax.shard_map(local_step, mesh=mesh, in_specs=(tok_spec, tok_spec, tok_spec, tok_spec, tok_spec, w_spec, w_spec, w_spec), out_specs=(tok_spec, grad_spec, grad_spec, grad_spec), check_vma=False)
```

profile of v0, /device:TPU:112, one launch (start us, length us, event | category | flops | bytes accessed | tf_op | source)
XLA Modules:
  0.0 162.4 jit_solution(3352098756402670646)
XLA Ops:
  0.6 0.8 compare_and_fusion.1
  1.5 0.1 reshape.71
  1.6 2.4 %scatter_custom_fusion = s32[960]{0:T(1024)S(1)} fusion(s32[512]{0:T(512)S(1)} %bitcast.51, s32[512]{0:T(512)S(1)} %iota.3, s32[]{:T(128)} %constant.58.clone.1), kind=kCustom, calls=%fused_computation.45 | custom fusion | bytes 3844 | tf_op jit(solution)/shard_map/scatter | solution.py:16
  4.1 4.4 %gather_fusion.3 = bf16[960,1536]{1,0:T(8,128)(2,1)S(1)} fusion(bf16[64,1536]{1,0:T(8,128)(2,1)S(1)} %copy-done, s32[1024]{0:T(1024)S(1)} %pad_clamp_fusion.1), kind=kCustom, calls=%fused_computation.1.clone | custom fusion | bytes 5902080 | tf_op jit(solution)/shard_map/jit(_take)/gather | solution.py:18
  8.5 1.9 %broadcast_select_fusion = bf16[960,1536]{1,0:T(8,128)(2,1)} fusion(bf16[960,1536]{1,0:T(8,128)(2,1)S(1)} %gather_fusion.3, pred[960]{0:T(1024)(128)(4,1)S(1)} %get-tuple-element.7), kind=kLoop, calls=%fused_computation.10 | loop fusion | flops 1474560 | bytes 5899200 | tf_op jit(solution)/shard_map/jit(_take)/select_n | solution.py:18
  10.3 5.4 %all-to-all-start.1 = ((bf16[40,1,24,1536]{3,2,1,0:T(8,128)(2,1)}), bf16[40,1,24,1536]{3,2,1,0:T(8,128)(2,1)S(1)}, u32[]{:S(2)}, u32[]{:S(2)}) async-start(bf16[40,1,24,1536]{3,2,1,0:T(8,128)(2,1)} %bitcast.7), calls=%async_computation.1 | async-start | bytes 5898240 | tf_op jit(solution)/shard_map/all_to_all | solution.py:57
  15.9 0.1 reshape.72
  16.0 5.5 %gather_fusion.2 = bf16[960,1536]{1,0:T(8,128)(2,1)} fusion(bf16[64,1536]{1,0:T(8,128)(2,1)S(1)} %copy-done.2, s32[1024]{0:T(1024)S(1)} %pad_clamp_fusion.1), kind=kCustom, calls=%fused_computation.clone | custom fusion | bytes 5902080 | tf_op jit(solution)/shard_map/jit(_take)/gather | solution.py:19
  21.5 6.5 %gather_fusion = f32[960]{0:T(1024)S(1)} fusion(f32[512]{0:T(512)S(1)} %reshape.72, s32[1024]{0:T(1024)S(1)} %pad_clamp_fusion.2), kind=kCustom, calls=%fused_computation.2 | custom fusion | bytes 11520 | tf_op jit(solution)/shard_map/jit(_take)/gather | solution.py:20
  28.0 3.5 %multiply_convert_fusion = bf16[960,1536]{1,0:T(8,128)(2,1)} fusion(bf16[960,1536]{1,0:T(8,128)(2,1)} %gather_fusion.2, f32[960]{0:T(1024)S(1)} %and_select_fusion, pred[960]{0:T(1024)(128)(4,1)S(1)} %get-tuple-element.7), kind=kLoop, calls=%fused_computation.6 | loop fusion | flops 5898240 | bytes 5903040 | tf_op jit(solution)/shard_map/convert_element_type | solution.py:21
  31.5 20.6 %all-to-all-done.1 = bf16[40,1,24,1536]{3,2,1,0:T(8,128)(2,1)S(1)} async-done(((bf16[40,1,24,1536]{3,2,1,0:T(8,128)(2,1)}), bf16[40,1,24,1536]{3,2,1,0:T(8,128)(2,1)S(1)}, u32[]{:S(2)}, u32[]{:S(2)}) %all-to-all-start.1) | async-done | bytes 2949152 | tf_op jit(solution)/shard_map/all_to_all | solution.py:57
  52.1 4.8 %all-to-all-start = ((bf16[40,1,24,1536]{3,2,1,0:T(8,128)(2,1)}), bf16[40,1,24,1536]{3,2,1,0:T(8,128)(2,1)}, u32[]{:S(2)}, u32[]{:S(2)}) async-start(bf16[40,1,24,1536]{3,2,1,0:T(8,128)(2,1)} %bitcast.49), calls=%async_computation | async-start | bytes 5898240 | tf_op jit(solution)/shard_map/all_to_all | solution.py:58
  56.9 0.3 copy.27
  57.2 6.1 %convolution_convert_fusion = bf16[5,192,512]{2,1,0:T(8,128)(2,1)S(1)} fusion(bf16[5,192,1536]{2,1,0:T(8,128)(2,1)S(1)} %bitcast.40, bf16[5,1536,512]{2,1,0:T(8,128)(2,1)} %param.15), kind=kOutput, calls=%fused_computation.24 | convolution fusion | flops 1510440960 | bytes 11796480 | tf_op jit(solution)/shard_map/erd,edf->erf/dot_general | solution.py:32
  63.4 0.1 slice-done.3
  63.5 2.7 %convolution_convert_fusion.1 = bf16[5,192,512]{2,1,0:T(8,128)(2,1)} fusion(bf16[5,192,1536]{2,1,0:T(8,128)(2,1)S(1)} %bitcast.41, bf16[5,1536,512]{2,1,0:T(8,128)(2,1)S(1)} %bitcast.53), kind=kOutput, calls=%fused_computation.25 | convolution fusion | flops 1510440960 | bytes 11796480 | tf_op jit(solution)/shard_map/erd,edf->erf/dot_general | solution.py:33
  66.2 26.6 %all-to-all-done = bf16[40,1,24,1536]{3,2,1,0:T(8,128)(2,1)} async-done(((bf16[40,1,24,1536]{3,2,1,0:T(8,128)(2,1)}), bf16[40,1,24,1536]{3,2,1,0:T(8,128)(2,1)}, u32[]{:S(2)}, u32[]{:S(2)}) %all-to-all-start) | async-done | bytes 2949152 | tf_op jit(solution)/shard_map/all_to_all | solution.py:58
  92.8 2.3 %copy.25 = bf16[5,8,1,24,1536]{4,3,1,0,2:T(8,128)(2,1)S(1)} copy(bf16[5,8,1,24,1536]{4,3,0,1,2:T(8,128)(2,1)} %bitcast.4) | data formatting | bytes 5898240 | tf_op jit(solution)/shard_map/all_to_all | solution.py:58
  95.1 7.3 %fusion.2 = (bf16[5,192,512]{2,1,0:T(8,128)(2,1)S(1)}, f32[5,192,512]{2,1,0:T(8,128)S(1)}) fusion(bf16[5,192,512]{2,1,0:T(8,128)(2,1)S(1)} %copy-done.12, bf16[5,192,512]{2,1,0:T(8,128)(2,1)S(1)} %convolution_convert_fusion, bf16[5,192,1536]{2,1,0:T(8,128)(2,1)S(1)} %bitcast.46, bf16[5,512,1536]{2,1,0:T(8,128)(2,1)} %param.16), kind=kOutput, calls=%fused_computation.15 | convolution fusion | flops 1515847680 | bytes 15728640 | tf_op jit(solution)/shard_map/erd,efd->erf/dot_general | solution.py:37
  102.5 2.7 %fusion.17 = f32[5,192,1536]{2,1,0:T(8,128)S(1)} fusion(bf16[5,192,512]{2,1,0:T(8,128)(2,1)S(1)} %get-tuple-element.9, bf16[5,1536,512]{2,1,0:T(8,128)(2,1)S(1)} %bitcast.45), kind=kOutput, calls=%fused_computation.49 | convolution fusion | flops 1509949440 | bytes 14745600 | tf_op jit(solution)/shard_map/erf,edf->erd/dot_general | solution.py:43
  105.2 7.6 %add_convert_fusion = bf16[5,192,1536]{2,1,0:T(8,128)(2,1)} fusion(f32[5,192,1536]{2,1,0:T(8,128)S(1)} %fusion.17, bf16[5,1536,512]{2,1,0:T(8,128)(2,1)} %param.17, f32[5,192,512]{2,1,0:T(8,128)S(1)} %get-tuple-element.10, bf16[5,192,512]{2,1,0:T(8,128)(2,1)S(1)} %convolution_convert_fusion), kind=kOutput, calls=%fused_computation.5 | convolution fusion | flops 1516339200 | bytes 19660800 | tf_op jit(solution)/shard_map/erf,edf->erd/dot_general | solution.py:43
  112.9 3.6 %copy.28 = bf16[5,8,24,1536]{3,2,0,1:T(8,128)(2,1)} copy(bf16[5,8,24,1536]{3,2,1,0:T(8,128)(2,1)} %bitcast.50) | data formatting | bytes 5898240 | tf_op jit(solution)/shard_map/reshape | solution.py:60
  116.5 4.1 %all-to-all-start.2 = ((bf16[5,8,24,1536]{3,2,0,1:T(8,128)(2,1)}), bf16[5,8,24,1536]{3,2,0,1:T(8,128)(2,1)S(1)}, u32[]{:S(2)}, u32[]{:S(2)}) async-start(bf16[5,8,24,1536]{3,2,0,1:T(8,128)(2,1)} %copy.28), calls=%async_computation.2 | async-start | bytes 5898240 | tf_op jit(solution)/shard_map/all_to_all | solution.py:60
  120.6 0.1 copy.21
  120.7 0.1 copy.29
  120.8 0.1 reshape.102
  120.9 10.4 %fusion.18 = f32[5,1536,512]{2,1,0:T(8,128)} fusion(bf16[5,192,1536]{2,1,0:T(8,128)(2,1)} %bitcast.42, bf16[5,192,512]{2,1,0:T(8,128)(2,1)} %copy-done.7), kind=kOutput, calls=%fused_computation.50 | convolution fusion | flops 1509949440 | bytes 19660800 | tf_op jit(solution)/shard_map/erd,erf->edf/dot_general | solution.py:41
  131.4 8.1 %fusion.9 = f32[5,512,1536]{2,1,0:T(8,128)} fusion(bf16[5,192,1536]{2,1,0:T(8,128)(2,1)S(1)} %bitcast.47, bf16[5,192,512]{2,1,0:T(8,128)(2,1)S(1)} %copy-done.13, bf16[5,192,512]{2,1,0:T(8,128)(2,1)S(1)} %copy-done.9), kind=kOutput, calls=%fused_computation.26 | convolution fusion | flops 1513881600 | bytes 20643840 | tf_op jit(solution)/shard_map/erf,erd->efd/dot_general | solution.py:40
  139.5 8.1 %fusion.16 = f32[5,1536,512]{2,1,0:T(8,128)} fusion(bf16[5,192,1536]{2,1,0:T(8,128)(2,1)S(1)} %bitcast.43, f32[5,192,512]{2,1,0:T(8,128)S(1)} %copy-done.11, bf16[5,192,512]{2,1,0:T(8,128)(2,1)S(1)} %copy-done.9), kind=kOutput, calls=%fused_computation.48 | convolution fusion | flops 1513390080 | bytes 21626880 | tf_op jit(solution)/shard_map/erd,erf->edf/dot_general | solution.py:42
  147.6 8.9 %all-to-all-done.2 = bf16[5,8,24,1536]{3,2,0,1:T(8,128)(2,1)S(1)} async-done(((bf16[5,8,24,1536]{3,2,0,1:T(8,128)(2,1)}), bf16[5,8,24,1536]{3,2,0,1:T(8,128)(2,1)S(1)}, u32[]{:S(2)}, u32[]{:S(2)}) %all-to-all-start.2) | async-done | bytes 2949152 | tf_op jit(solution)/shard_map/all_to_all | solution.py:60
  156.5 3.0 %gather_fusion.1 = bf16[512,1536]{1,0:T(8,128)(2,1)} fusion(bf16[960,1536]{1,0:T(8,128)(2,1)S(1)} %bitcast.39, s32[1024]{0:T(1024)S(1)} %pad_clamp_fusion), kind=kCustom, calls=%fused_computation.3 | custom fusion | bytes 3147776 | tf_op jit(solution)/shard_map/jit(_take)/gather | solution.py:27
  159.5 2.9 %fusion.8 = bf16[64,1536]{1,0:T(8,128)(2,1)} fusion(bf16[512,1536]{1,0:T(8,128)(2,1)} %gather_fusion.1, pred[64,8]{1,0:T(8,128)(4,1)S(1)} %copy.21), kind=kLoop, calls=%fused_computation.23 | loop fusion | flops 1474560 | bytes 1769984 | tf_op jit(solution)/shard_map/reduce_sum | solution.py:28
  (50 shorter events, 0.3 us)
Async XLA Ops:
  0.6 3.5 %copy-start = (bf16[64,1536]{1,0:T(8,128)(2,1)S(1)}, bf16[64,1536]{1,0:T(8,128)(2,1)}, u32[]{:S(2)}) copy-start(bf16[64,1536]{1,0:T(8,128)(2,1)} %param.10) | copy-start | bytes 589828
  10.3 5.4 %copy-start.14 = (f32[64,8]{0,1:T(8,128)S(1)}, f32[64,8]{0,1:T(8,128)}, u32[]{:S(2)}) copy-start(f32[64,8]{0,1:T(8,128)} %param.13) | copy-start | bytes 6148
  10.3 5.6 %copy-start.2 = (bf16[64,1536]{1,0:T(8,128)(2,1)S(1)}, bf16[64,1536]{1,0:T(8,128)(2,1)}, u32[]{:S(2)}) copy-start(bf16[64,1536]{1,0:T(8,128)(2,1)} %param.11) | copy-start | bytes 589828
  10.3 41.7 %all-to-all-start.1 = ((bf16[40,1,24,1536]{3,2,1,0:T(8,128)(2,1)}), bf16[40,1,24,1536]{3,2,1,0:T(8,128)(2,1)S(1)}, u32[]{:S(2)}, u32[]{:S(2)}) async-start(bf16[40,1,24,1536]{3,2,1,0:T(8,128)(2,1)} %bitcast.7), calls=%async_computation.1 | async-start | bytes 5898240 | tf_op jit(solution)/shard_map/all_to_all | solution.py:57
  52.1 40.7 %all-to-all-start = ((bf16[40,1,24,1536]{3,2,1,0:T(8,128)(2,1)}), bf16[40,1,24,1536]{3,2,1,0:T(8,128)(2,1)}, u32[]{:S(2)}, u32[]{:S(2)}) async-start(bf16[40,1,24,1536]{3,2,1,0:T(8,128)(2,1)} %bitcast.49), calls=%async_computation | async-start | bytes 5898240 | tf_op jit(solution)/shard_map/all_to_all | solution.py:58
  56.9 6.5 %slice-start.2 = ((s8[7864320]{0:T(1024)(128)(4,1)}), s8[4194304]{0:T(1024)(128)(4,1)S(1)}, s32[]{:S(2)}) async-start(s8[7864320]{0:T(1024)(128)(4,1)} %bitcast.52), calls=%async_computation.5 | async-start | bytes 8388608
  57.2 6.2 %copy-start.3 = (bf16[5,8,1,24,1536]{4,3,1,0,2:T(8,128)(2,1)}, bf16[5,8,1,24,1536]{4,3,1,0,2:T(8,128)(2,1)S(1)}, u32[]{:S(2)}) copy-start(bf16[5,8,1,24,1536]{4,3,1,0,2:T(8,128)(2,1)S(1)} %copy.27) | copy-start | bytes 8847364
  57.2 6.3 %slice-start.3 = ((s8[7864320]{0:T(1024)(128)(4,1)}), s8[3670016]{0:T(1024)(128)(4,1)S(1)}, s32[]{:S(2)}) async-start(s8[7864320]{0:T(1024)(128)(4,1)} %bitcast.52), calls=%async_computation.6 | async-start | bytes 7340032
  63.5 41.7 %copy-start.8 = (bf16[5,192,512]{2,1,0:T(8,128)(2,1)}, bf16[5,192,512]{2,1,0:T(8,128)(2,1)S(1)}, u32[]{:S(2)}) copy-start(bf16[5,192,512]{2,1,0:T(8,128)(2,1)S(1)} %convolution_convert_fusion) | copy-start | bytes 2949124
  92.8 2.3 %copy-start.12 = (bf16[5,192,512]{2,1,0:T(8,128)(2,1)S(1)}, bf16[5,192,512]{2,1,0:T(8,128)(2,1)}, u32[]{:S(2)}) copy-start(bf16[5,192,512]{2,1,0:T(8,128)(2,1)} %convolution_convert_fusion.1) | copy-start | bytes 2949124
  92.8 9.6 %slice-start = ((s8[7864320]{0:T(1024)(128)(4,1)}), s8[4194304]{0:T(1024)(128)(4,1)S(1)}, s32[]{:S(2)}) async-start(s8[7864320]{0:T(1024)(128)(4,1)} %bitcast.44), calls=%async_computation.3 | async-start | bytes 8388608
  95.1 7.3 %copy-start.5 = (bf16[5,8,1,24,1536]{4,3,1,0,2:T(8,128)(2,1)}, bf16[5,8,1,24,1536]{4,3,1,0,2:T(8,128)(2,1)S(1)}, u32[]{:S(2)}) copy-start(bf16[5,8,1,24,1536]{4,3,1,0,2:T(8,128)(2,1)S(1)} %copy.25) | copy-start | bytes 8847364
  95.1 7.4 %slice-start.1 = ((s8[7864320]{0:T(1024)(128)(4,1)}), s8[3670016]{0:T(1024)(128)(4,1)S(1)}, s32[]{:S(2)}) async-start(s8[7864320]{0:T(1024)(128)(4,1)} %bitcast.44), calls=%async_computation.4 | async-start | bytes 7340032
  102.4 2.8 %copy-start.7 = (bf16[5,192,512]{2,1,0:T(8,128)(2,1)}, bf16[5,192,512]{2,1,0:T(8,128)(2,1)S(1)}, u32[]{:S(2)}) copy-start(bf16[5,192,512]{2,1,0:T(8,128)(2,1)S(1)} %get-tuple-element.9) | copy-start | bytes 2949124
  102.4 2.8 %copy-start.10 = (f32[5,192,512]{2,1,0:T(8,128)}, f32[5,192,512]{2,1,0:T(8,128)S(1)}, u32[]{:S(2)}) copy-start(f32[5,192,512]{2,1,0:T(8,128)S(1)} %get-tuple-element.10) | copy-start | bytes 5898244
  116.5 39.9 %all-to-all-start.2 = ((bf16[5,8,24,1536]{3,2,0,1:T(8,128)(2,1)}), bf16[5,8,24,1536]{3,2,0,1:T(8,128)(2,1)S(1)}, u32[]{:S(2)}, u32[]{:S(2)}) async-start(bf16[5,8,24,1536]{3,2,0,1:T(8,128)(2,1)} %copy.28), calls=%async_computation.2 | async-start | bytes 5898240 | tf_op jit(solution)/shard_map/all_to_all | solution.py:60
  120.9 10.4 %copy-start.6 = (bf16[5,8,1,24,1536]{4,3,1,0,2:T(8,128)(2,1)S(1)}, bf16[5,8,1,24,1536]{4,3,1,0,2:T(8,128)(2,1)}, u32[]{:S(2)}) copy-start(bf16[5,8,1,24,1536]{4,3,1,0,2:T(8,128)(2,1)} %copy-done.5) | copy-start | bytes 8847364
  120.9 10.4 %copy-start.9 = (bf16[5,192,512]{2,1,0:T(8,128)(2,1)S(1)}, bf16[5,192,512]{2,1,0:T(8,128)(2,1)}, u32[]{:S(2)}) copy-start(bf16[5,192,512]{2,1,0:T(8,128)(2,1)} %copy-done.8) | copy-start | bytes 2949124
  120.9 10.4 %copy-start.13 = (bf16[5,192,512]{2,1,0:T(8,128)(2,1)S(1)}, bf16[5,192,512]{2,1,0:T(8,128)(2,1)}, u32[]{:S(2)}) copy-start(bf16[5,192,512]{2,1,0:T(8,128)(2,1)} %convolution_convert_fusion.1) | copy-start | bytes 2949124
  131.3 8.1 %copy-start.4 = (bf16[5,8,1,24,1536]{4,3,1,0,2:T(8,128)(2,1)S(1)}, bf16[5,8,1,24,1536]{4,3,1,0,2:T(8,128)(2,1)}, u32[]{:S(2)}) copy-start(bf16[5,8,1,24,1536]{4,3,1,0,2:T(8,128)(2,1)} %copy-done.3) | copy-start | bytes 8847364
  131.3 8.1 %copy-start.11 = (f32[5,192,512]{2,1,0:T(8,128)S(1)}, f32[5,192,512]{2,1,0:T(8,128)}, u32[]{:S(2)}) copy-start(f32[5,192,512]{2,1,0:T(8,128)} %copy-done.10) | copy-start | bytes 5898244
  156.5 5.9 %copy-start.1 = (bf16[64,1536]{1,0:T(8,128)(2,1)S(1)}, bf16[64,1536]{1,0:T(8,128)(2,1)}, u32[]{:S(2)}) copy-start(bf16[64,1536]{1,0:T(8,128)(2,1)} %param.10) | copy-start | bytes 589828
where the time goes:
time: 163 us; the launch traced here: 162 us
  waiting for transfers between devices  56.1 us (34%)
  matrix products  53.1 us (33%)
  local copies, waits for them, and re-layouts  28.8 us (18%)
  starting transfers between devices  14.3 us (9%)
  other arithmetic  9.06 us (6%)
    all_to_all x1, waiting for transfers between devices, local_step(): lax.all_to_all(dz_send.reshape(n_exp, 1, cap_rows, d_model), 'ep', 0, 1,...  26.6 us
    all_to_all x1, waiting for transfers between devices, local_step(): lax.all_to_all(x_send.reshape(n_exp, 1, cap_rows, d_model), 'ep', 0, 1, t...  20.6 us
    dot_general x1, matrix products, expert_backward(): jnp.einsum('erd,erf->edf', x_rows, d_gate, preferred_element_type=jnp.flo...  10.4 us
    all_to_all x1, waiting for transfers between devices, local_step(): lax.all_to_all(dx_rows.reshape(n_local, n_dev, cap_rows, d_model), 'ep',...  8.88 us
    dot_general x1, matrix products, expert_backward(): jnp.einsum('erd,erf->edf', x_rows, d_up, preferred_element_type=jnp.float32)  8.14 us
    dot_general x1, matrix products, expert_backward(): jnp.einsum('erf,erd->efd', hidden, dz_rows, preferred_element_type=jnp.fl...  8.1 us
    dot_general x1, matrix products, expert_backward(): jnp.einsum('erf,edf->erd', d_up, w_up, preferred_element_type=jnp.float32)  7.64 us
    dot_general x1, matrix products, expert_backward(): jnp.einsum('erd,efd->erf', dz_rows, w_down, preferred_element_type=jnp.fl...  7.29 us
  transfers between devices with their start and end apart: 3, of which 3 were waited for; matrix products, arithmetic and copies ran while one was open for 32% of the time, Pallas kernels for 0%

commit v1 on v0

v1 whole, which is shorter than its diff:
```python
import functools

import jax
import jax.numpy as jnp
from jax import lax
from jax.experimental import pallas as pl
from jax.experimental.pallas import tpu as pltpu
from jax.sharding import PartitionSpec as P

F32 = jnp.float32
BF16 = jnp.bfloat16
NT = (((1,), (1,)), ((), ()))
TN = (((0,), (0,)), ((), ()))
DY_Q = 3
DX_Q = 3
KEY_STRIDE = 256


def slot_capacity(tok_dev, top_k, n_exp):
    return ((3 * tok_dev * top_k) // (2 * n_exp) + 7) // 8 * 8


def exchange_kernel(
    n_dev, cap,
    x_hbm, dy_hbm, meta_hbm, w1_hbm, w3_hbm, w2_hbm,
    xbuf_o, dz_o, h_o, da_o, db_o, r1_o, l1_o, ra_o, lb_o, own_o,
    xg, dyg, mt, w1, w3, w2, xb, dz, hh, qq, uu, bb, dh, da, db, dxq,
    pm, pt, gm, part, sibr, sums,
    loc_sem, w_sem, out_sem, s_sem, send, recv,
):
    n_exp = w1_hbm.shape[0]
    tok, d = x_hbm.shape
    half = tok // 2
    n_chip = n_dev // 2
    rc_rows = 2 * cap
    used = n_exp * rc_rows
    me = lax.axis_index("ep")
    chip, core = me // 2, lax.rem(me, 2)
    right = lax.rem(chip + 1, n_chip) * 2 + core
    left = lax.rem(chip + n_chip - 1, n_chip) * 2 + core
    sib = chip * 2 + 1 - core

    counter = [0]

    def remote(src, dst, dev):
        i = counter[0]
        counter[0] += 1
        return pltpu.make_async_remote_copy(
            src_ref=src, dst_ref=dst, send_sem=send.at[i], recv_sem=recv.at[i],
            device_id={"ep": dev}, device_id_type=pl.DeviceIdType.MESH)

    started = []

    def go(copy):
        copy.start()
        started.append(copy)
        return copy

    loc = [
        pltpu.make_async_copy(meta_hbm, mt.at[0, 0], loc_sem.at[0]),
        pltpu.make_async_copy(x_hbm, xg.at[0, 0], loc_sem.at[1]),
        pltpu.make_async_copy(dy_hbm, dyg.at[0, 0], loc_sem.at[2]),
    ]
    for c in loc:
        c.start()
    wcopies = {}
    for k, (src, dst) in enumerate(((w1_hbm, w1), (w3_hbm, w3), (w2_hbm, w2))):
        for e in range(n_exp):
            wcopies[k, e] = pltpu.make_async_copy(src.at[e], dst.at[e], w_sem.at[k * n_exp + e])
    for e in range(n_exp):
        wcopies[0, e].start()
        wcopies[1, e].start()
    for e in range(n_exp):
        wcopies[2, e].start()

    barrier = pltpu.get_barrier_semaphore()
    for dev in (right, left, sib):
        pl.semaphore_signal(barrier, inc=1, device_id={"ep": dev}, device_id_type=pl.DeviceIdType.MESH)
    pl.semaphore_wait(barrier, 3)

    lo, hi = pl.ds(0, half), pl.ds(half, half)
    loc[0].wait()
    m_r = go(remote(mt.at[0, 0], mt.at[3, 0], right))
    m_l = go(remote(mt.at[0, 0], mt.at[1, 0], left))
    m_s = go(remote(mt.at[0, 0], mt.at[0, 1], sib))
    loc[1].wait()
    xa_r = go(remote(xg.at[0, 0, lo], xg.at[3, 0, lo], right))
    xb_l = go(remote(xg.at[0, 0, hi], xg.at[1, 0, hi], left))
    xb_r = go(remote(xg.at[0, 0, hi], xg.at[3, 0, hi], right))
    xa_l = go(remote(xg.at[0, 0, lo], xg.at[1, 0, lo], left))
    x_s = go(remote(xg.at[0, 0], xg.at[0, 1], sib))
    m_r.wait_recv()
    m_rr = go(remote(mt.at[3, 0], mt.at[2, 0], right))
    m_s3 = go(remote(mt.at[3, 0], mt.at[3, 1], sib))
    m_l.wait_recv()
    m_s1 = go(remote(mt.at[1, 0], mt.at[1, 1], sib))
    xa_r.wait_recv()
    xa_rr = go(remote(xg.at[3, 0, lo], xg.at[2, 0, lo], right))
    xb_l.wait_recv()
    xb_ll = go(remote(xg.at[1, 0, hi], xg.at[2, 0, hi], left))

    loc[2].wait()
    qd = d // DY_Q
    dcol = [pl.ds(q * qd, qd) for q in range(DY_Q)]
    dy = {}

    def dy_own(q):
        c = dcol[q]
        dy["ar", q] = go(remote(dyg.at[0, 0, lo, c], dyg.at[3, 0, lo, c], right))
        dy["bl", q] = go(remote(dyg.at[0, 0, hi, c], dyg.at[1, 0, hi, c], left))
        dy["br", q] = go(remote(dyg.at[0, 0, hi, c], dyg.at[3, 0, hi, c], right))
        dy["al", q] = go(remote(dyg.at[0, 0, lo, c], dyg.at[1, 0, lo, c], left))
        dy["s0", q] = go(remote(dyg.at[0, 0, :, c], dyg.at[0, 1, :, c], sib))

    def dy_relay(q):
        c = dcol[q]
        dy["ar", q].wait_recv()
        dy["arr", q] = go(remote(dyg.at[3, 0, lo, c], dyg.at[2, 0, lo, c], right))
        dy["bl", q].wait_recv()
        dy["bll", q] = go(remote(dyg.at[1, 0, hi, c], dyg.at[2, 0, hi, c], left))
        dy["br", q].wait_recv()
        dy["s3", q] = go(remote(dyg.at[3, 0, :, c], dyg.at[3, 1, :, c], sib))
        dy["al", q].wait_recv()
        dy["s1", q] = go(remote(dyg.at[1, 0, :, c], dyg.at[1, 1, :, c], sib))

    def dy_far(q):
        c = dcol[q]
        dy["arr", q].wait_recv()
        dy["bll", q].wait_recv()
        dy["s2", q] = go(remote(dyg.at[2, 0, :, c], dyg.at[2, 1, :, c], sib))

    dy_own(0)
    dy_own(1)

    rows_i = lax.broadcasted_iota(jnp.int32, (KEY_STRIDE, 2 * tok), 0)
    lane_i = lax.broadcasted_iota(jnp.int32, (16, 2 * tok), 1)
    row_key = (rows_i + me * KEY_STRIDE).astype(F32)

    def build(s):
        m0, m1 = mt[s, 0], mt[s, 1]
        first = lane_i < tok
        keys = jnp.where(first, m0, m1 + float(cap))
        gates = jnp.where(first, m0, m1)
        ones = jnp.zeros((KEY_STRIDE, 2 * tok), F32)
        gmat = jnp.zeros((KEY_STRIDE, 2 * tok), F32)
        for j in range(8):
            hit = row_key == keys[j:j + 1, :]
            ones = jnp.where(hit, 1.0, ones)
            gmat = jnp.where(hit, gates[8 + j:9 + j, :], gmat)
        pm[s] = ones.astype(BF16)
        pt[s] = jnp.transpose(ones).astype(BF16)
        gm[s] = jnp.sum(gmat, axis=1, keepdims=True)

    m_s.wait_recv()
    build(0)
    m_s3.wait_recv()
    build(3)
    m_s1.wait_recv()
    build(1)
    m_rr.wait_recv()
    m_s2 = go(remote(mt.at[2, 0], mt.at[2, 1], sib))

    def gather_x(s):
        src = xg[s].reshape(2 * tok, d)
        rows = jnp.dot(pm[s, :used, :], src, preferred_element_type=F32).astype(BF16)
        for e in range(n_exp):
            xb[e, s * rc_rows:(s + 1) * rc_rows, :] = rows[e * rc_rows:(e + 1) * rc_rows, :]

    xb_r.wait_recv()
    x_s3 = go(remote(xg.at[3, 0], xg.at[3, 1], sib))
    xa_l.wait_recv()
    x_s1 = go(remote(xg.at[1, 0], xg.at[1, 1], sib))
    x_s.wait_recv()
    gather_x(0)
    x_s3.wait_recv()
    gather_x(3)
    m_s2.wait_recv()
    build(2)
    x_s1.wait_recv()
    gather_x(1)
    xa_rr.wait_recv()
    xb_ll.wait_recv()
    x_s2 = go(remote(xg.at[2, 0], xg.at[2, 1], sib))
    x_s2.wait_recv()
    gather_x(2)

    outs = []

    def put(src, dst):
        i = len(outs)
        c = pltpu.make_async_copy(src, dst, out_sem.at[i])
        c.start()
        outs.append(c)

    def up(e):
        wcopies[0, e].wait()
        wcopies[1, e].wait()
        x = xb[e]
        a16 = jnp.dot(x, w1[e], preferred_element_type=F32).astype(BF16)
        b16 = jnp.dot(x, w3[e], preferred_element_type=F32).astype(BF16)
        a = a16.astype(F32)
        b = b16.astype(F32)
        sg = jax.nn.sigmoid(a)
        silu = a * sg
        hh[e] = (silu * b).astype(BF16)
        uu[e] = silu
        qq[e] = sg * (1.0 + a * (1.0 - sg))
        bb[e] = b16

    put(xb, xbuf_o)
    for e in range(n_exp):
        up(e)
        if e == 0:
            dy_relay(0)
            dy_own(2)
        if e == 2:
            dy_relay(1)
    put(hh, h_o)
    dy_far(0)

    def gather_dy(q):
        c = slice(q * qd, (q + 1) * qd)
        for s, key in ((0, "s0"), (3, "s3"), (1, "s1"), (2, "s2")):
            dy[key, q].wait_recv()
            src = dyg[s, :, :, c].reshape(2 * tok, qd)
            rows = jnp.dot(pm[s, :used, :], src, preferred_element_type=F32)
            rows = (rows * gm[s, :used, :]).astype(BF16)
            for e in range(n_exp):
                dz[e, s * rc_rows:(s + 1) * rc_rows, c] = rows[e * rc_rows:(e + 1) * rc_rows, :]

    def down(e, q):
        c = slice(q * qd, (q + 1) * qd)
        if q == 0:
            wcopies[2, e].wait()
        val = lax.dot_general(dz[e, :, c], w2[e, :, c], NT, preferred_element_type=F32)
        if q > 0:
            val = val + dh[e]
        if q < DY_Q - 1:
            dh[e] = val
        else:
            da[e] = (val * bb[e].astype(F32) * qq[e]).astype(BF16)
            db[e] = (val * uu[e]).astype(BF16)

    for q in range(DY_Q):
        if q == 0:
            dy_relay(2)
        if q == 1:
            dy_far(1)
        if q == 2:
            dy_far(2)
        gather_dy(q)
        for e in range(n_exp):
            down(e, q)
    put(dz, dz_o)
    put(da, da_o)
    put(db, db_o)

    qx = d // DX_Q
    sib_copies = []

    def dx_block(q):
        c = slice(q * qx, (q + 1) * qx)
        for e in range(n_exp):
            v = lax.dot_general(da[e], w1[e, c, :], NT, preferred_element_type=F32)
            v = v + lax.dot_general(db[e], w3[e, c, :], NT, preferred_element_type=F32)
            dxq[e] = v.astype(BF16)
        for s in range(n_chip):
            rows = dxq[:, s * rc_rows:(s + 1) * rc_rows, :].reshape(used, qx)
            part[q, s] = jnp.dot(pt[s, :, :used], rows, preferred_element_type=F32).reshape(2, tok, qx)
        sib_copies.append(go(remote(part.at[q, :, 1], sibr.at[q], sib)))

    def finish(q):
        c = slice(q * qx, (q + 1) * qx)
        sib_copies[q].wait_recv()
        for s in range(n_chip):
            sums[s, :, c] = part[q, s, 0] + sibr[q, s]

    for q in range(DX_Q):
        dx_block(q)
        if q > 0:
            finish(q - 1)
    finish(DX_Q - 1)

    put(sums.at[2, lo], r1_o.at[lo])
    put(sums.at[1, hi], r1_o.at[hi])
    put(sums.at[3, lo], l1_o.at[lo])
    put(sums.at[2, hi], l1_o.at[hi])
    put(sums.at[1, lo], ra_o)
    put(sums.at[3, hi], lb_o)
    put(sums.at[0], own_o)
    for c in outs:
        c.wait()
    for c in started:
        c.wait_send()


def run_exchange(x, dy, meta, w1, w3, w2, n_dev, cap):
    n_exp, d, f = w1.shape
    tok = x.shape[0]
    half = tok // 2
    n_chip = n_dev // 2
    rows = n_dev * cap
    used = n_exp * 2 * cap
    qx = d // DX_Q
    any_spec = pl.BlockSpec(memory_space=pl.ANY)
    sds = jax.ShapeDtypeStruct
    outs = (
        sds((n_exp, rows, d), BF16), sds((n_exp, rows, d), BF16),
        sds((n_exp, rows, f), BF16), sds((n_exp, rows, f), BF16), sds((n_exp, rows, f), BF16),
        sds((tok, d), F32), sds((tok, d), F32), sds((half, d), F32), sds((half, d), F32), sds((tok, d), F32),
    )
    n_copies = 80
    scratch = [
        pltpu.VMEM((n_chip, 2, tok, d), BF16),
        pltpu.VMEM((n_chip, 2, tok, d), BF16),
        pltpu.VMEM((n_chip, 2, 16, 2 * tok), F32),
        pltpu.VMEM((n_exp, d, f), BF16),
        pltpu.VMEM((n_exp, d, f), BF16),
        pltpu.VMEM((n_exp, f, d), BF16),
        pltpu.VMEM((n_exp, rows, d), BF16),
        pltpu.VMEM((n_exp, rows, d), BF16),
        pltpu.VMEM((n_exp, rows, f), BF16),
        pltpu.VMEM((n_exp, rows, f), F32),
        pltpu.VMEM((n_exp, rows, f), F32),
        pltpu.VMEM((n_exp, rows, f), BF16),
        pltpu.VMEM((n_exp, rows, f), F32),
        pltpu.VMEM((n_exp, rows, f), BF16),
        pltpu.VMEM((n_exp, rows, f), BF16),
        pltpu.VMEM((n_exp, rows, qx), BF16),
        pltpu.VMEM((n_chip, KEY_STRIDE, 2 * tok), BF16),
        pltpu.VMEM((n_chip, 2 * tok, KEY_STRIDE), BF16),
        pltpu.VMEM((n_chip, KEY_STRIDE, 1), F32),
        pltpu.VMEM((DX_Q, n_chip, 2, tok, qx), F32),
        pltpu.VMEM((DX_Q, n_chip, tok, qx), F32),
        pltpu.VMEM((n_chip, tok, d), F32),
        pltpu.SemaphoreType.DMA((3,)),
        pltpu.SemaphoreType.DMA((3 * n_exp,)),
        pltpu.SemaphoreType.DMA((16,)),
        pltpu.SemaphoreType.DMA((1,)),
        pltpu.SemaphoreType.DMA((n_copies,)),
        pltpu.SemaphoreType.DMA((n_copies,)),
    ]
    return pl.pallas_call(
        functools.partial(exchange_kernel, n_dev, cap),
        out_shape=outs,
        in_specs=[any_spec] * 6,
        out_specs=(any_spec,) * len(outs),
        scratch_shapes=scratch,
        compiler_params=pltpu.CompilerParams(
            collective_id=0, has_side_effects=True, vmem_limit_bytes=64_000_000),
        name="exchange",
    )(x, dy, meta, w1, w3, w2)


def grad_in_kernel(x_ref, da_ref, db_ref, g1_ref, g3_ref):
    x = x_ref[0]
    g1_ref[0] = lax.dot_general(x, da_ref[0], TN, preferred_element_type=F32)
    g3_ref[0] = lax.dot_general(x, db_ref[0], TN, preferred_element_type=F32)


def grad_in(xb, da, db, blk=512):
    n_exp, rows, d = xb.shape
    f = da.shape[2]
    row_spec = pl.BlockSpec((1, rows, f), lambda e, k: (e, 0, 0))
    out_spec = pl.BlockSpec((1, blk, f), lambda e, k: (e, k, 0))
    out = jax.ShapeDtypeStruct((n_exp, d, f), F32)
    return pl.pallas_call(
        grad_in_kernel,
        grid=(n_exp, d // blk),
        out_shape=(out, out),
        in_specs=[pl.BlockSpec((1, rows, blk), lambda e, k: (e, 0, k)), row_spec, row_spec],
        out_specs=(out_spec, out_spec),
        cost_estimate=pl.CostEstimate(flops=4 * n_exp * rows * d * f, bytes_accessed=8 * n_exp * d * f, transcendentals=0),
        name="grad_in",
    )(xb, da, db)


def grad_out_kernel(h_ref, dz_ref, g_ref):
    g_ref[0] = lax.dot_general(h_ref[0], dz_ref[0], TN, preferred_element_type=F32)


def grad_out(h, dz, blk=256):
    n_exp, rows, f = h.shape
    d = dz.shape[2]
    return pl.pallas_call(
        grad_out_kernel,
        grid=(n_exp, f // blk),
        out_shape=jax.ShapeDtypeStruct((n_exp, f, d), F32),
        in_specs=[pl.BlockSpec((1, rows, blk), lambda e, k: (e, 0, k)), pl.BlockSpec((1, rows, d), lambda e, k: (e, 0, 0))],
        out_specs=pl.BlockSpec((1, blk, d), lambda e, k: (e, k, 0)),
        cost_estimate=pl.CostEstimate(flops=2 * n_exp * rows * d * f, bytes_accessed=4 * n_exp * d * f, transcendentals=0),
        name="grad_out",
    )(h, dz)


def solution(mesh):
    n_dev = mesh.shape["ep"]
    n_chip = n_dev // 2

    def local_step(x_loc, dy_loc, ids_loc, gate_loc, slot_loc, w_gate, w_down, w_up):
        tok, top_k = ids_loc.shape
        n_local = w_gate.shape[0]
        cap = slot_capacity(tok, top_k, n_local * n_dev)
        half = tok // 2
        keys = (ids_loc // n_local) * KEY_STRIDE + (ids_loc % n_local) * (2 * cap) + slot_loc
        keys = jnp.where(slot_loc >= 0, keys, -1000).astype(F32)
        meta = jnp.concatenate([keys.T, gate_loc.T], axis=0)
        meta = jnp.concatenate([meta, meta], axis=1)
        xb, dz, h, da, db, r1, l1, ra, lb, own = run_exchange(
            x_loc, dy_loc, meta, w_gate, w_up, w_down, n_dev, cap)
        to_right = [(c * 2 + k, (c + 1) % n_chip * 2 + k) for c in range(n_chip) for k in range(2)]
        to_left = [(b, a) for a, b in to_right]
        r1 = lax.ppermute(r1, "ep", to_right)
        l1 = lax.ppermute(l1, "ep", to_left)
        g_gate, g_up = grad_in(xb, da, db)
        g_gate, g_up, r1, l1 = lax.optimization_barrier((g_gate, g_up, r1, l1))
        r2 = lax.ppermute(ra + r1[:half], "ep", to_right)
        l2 = lax.ppermute(lb + l1[half:], "ep", to_left)
        g_down = grad_out(h, dz)
        dx_lo = own[:half] + l1[:half] + r2
        dx_hi = own[half:] + r1[half:] + l2
        dx = jnp.concatenate([dx_lo, dx_hi], axis=0).astype(BF16)
        return dx, g_gate, g_down, g_up

    tok_spec = P(("dp", "ep"), None)
    w_spec = P("ep", None, None)
    grad_spec = P(("dp", "ep"), None, None)
    return jax.shard_map(
        local_step, mesh=mesh,
        in_specs=(tok_spec,) * 5 + (w_spec,) * 3,
        out_specs=(tok_spec, grad_spec, grad_spec, grad_spec),
        check_vma=False)
```

time: 163 us -> 81.6 us (0.50)
  Pallas kernels: 0 us -> 71.7 us
  waiting for transfers between devices: 56.1 us -> 0.01 us
  matrix products: 53.1 us -> 0 us
  local copies, waits for them, and re-layouts: 28.8 us -> 0.01 us
  starting transfers between devices: 14.3 us -> 5.5 us
  other arithmetic: 9.06 us -> 2.96 us
    pallas_call x0 -> x3, Pallas kernels: none -> 71.7 us  [the longest x1 42.9 us: run_exchange(): pl.pallas_call(functools.partial(exchange_kernel, n_dev, cap), out_shape=...]
    all_to_all x3 -> x0, waiting for transfers between devices: 56.1 us -> none  [the longest x1 26.6 us: local_step(): lax.all_to_all(dz_send.reshape(n_exp, 1, cap_rows, d_model), 'ep', 0, 1,...]
    dot_general x8 -> x0, matrix products: 53.1 us -> none  [the longest x1 10.4 us: expert_backward(): jnp.einsum('erd,erf->edf', x_rows, d_gate, preferred_element_type=jnp.flo...]
    gather x4 -> x0, local copies, waits for them, and re-layouts: 19.3 us -> none  [the longest x1 6.52 us: source_dispatch(): jnp.take(gate_src.reshape(n_copy), slot_copy, mode='fill', fill_value=0)]
    all_to_all x3 -> x0, starting transfers between devices: 14.3 us -> none  [the longest x1 5.43 us: local_step(): lax.all_to_all(x_send.reshape(n_exp, 1, cap_rows, d_model), 'ep', 0, 1, t...]
    ppermute x0 -> x4, starting transfers between devices: none -> 5.5 us  [the longest x1 2.6 us: local_step(): l1 = lax.ppermute(l1, 'ep', to_left)]
    reshape x3 -> x0, local copies, waits for them, and re-layouts: 3.83 us -> none  [the longest x1 3.65 us: local_step(): dx_rows.reshape(n_local, n_dev, cap_rows, d_model)]
    convert_element_type x1 -> x0, other arithmetic: 3.46 us -> none  [source_dispatch(): dz_send = (gate_slot[:, None] * dy_send).astype(jnp.bfloat16)]
  transfers between devices with their start and end apart: 3 -> 4, of which waited for: 3 -> 0; matrix products, arithmetic and copies ran while one was open for 32% -> 0% of each run, Pallas kernels for 0% -> 36%
where the time goes in v1:
time: 81.6 us; the launch traced here: 80.9 us
  Pallas kernels  71.7 us (88%)
  starting transfers between devices  5.5 us (7%)
  other arithmetic  2.96 us (4%)
    pallas_call x1, Pallas kernels, run_exchange(): pl.pallas_call(functools.partial(exchange_kernel, n_dev, cap), out_shape=...  42.9 us
    pallas_call x1, Pallas kernels, grad_in(): pl.pallas_call(grad_in_kernel, grid=(n_exp, d // blk), out_shape=(out, ou...  17.3 us
    pallas_call x1, Pallas kernels, grad_out(): pl.pallas_call(grad_out_kernel, grid=(n_exp, f // blk), out_shape=jax.Sha...  11.5 us
    ppermute x1, starting transfers between devices, local_step(): l1 = lax.ppermute(l1, 'ep', to_left)  2.6 us
  transfers between devices with their start and end apart: 4, of which 0 were waited for; matrix products, arithmetic and copies ran while one was open for 0% of the time, Pallas kernels for 36%

profile of v1, /device:TPU:112, one launch (start us, length us, event | category | flops | bytes accessed | tf_op | source)
XLA Modules:
  0.0 80.9 jit_solution(13588285673294313295)
XLA Ops:
  0.6 0.7 fusion.5
  1.4 1.4 %maximum_maximum_fusion.meta_hbm = f32[16,128]{1,0:T(8,128)} fusion(f32[8,64]{1,0:T(8,128)} %bitcast.3, f32[8,64]{1,0:T(8,128)S(1)} %fusion.5), kind=kLoop, calls=%fused_computation.5 | loop fusion | flops 6144 | bytes 12288 | tf_op jit(solution)/shard_map/concatenate | solution.py:408
  2.8 42.9 %exchange.1 = (bf16[5,192,1536]{2,1,0:T(8,128)(2,1)}, bf16[5,192,1536]{2,1,0:T(8,128)(2,1)}, bf16[5,192,512]{2,1,0:T(8,128)(2,1)}, bf16[5,192,512]{2,1,0:T(8,128...) custom-call(bf16[64,1536]{1,0:T(8,128)(2,1)} %x_hbm.1, ...), custom_call_target="tpu_custom_call" | custom-call | tf_op jit(solution)/shard_map/exchange/pallas_call | solution.py:343
  45.7 0.0 copy-start.2
  45.7 0.0 copy-start.1
  45.7 0.7 collective-permute-start
  46.4 2.6 %collective-permute-start.1 = (f32[64,1536]{1,0:T(8,128)}, f32[64,1536]{1,0:T(8,128)S(1)}, u32[]{:S(2)}, u32[]{:S(2)}) collective-permute-start(f32[64,1536]{1,0:T(8,128)} %get-tuple-element.27), channel_id=1, source_target_pairs={{2,0},{3,1},{4,2},{5,3},{6,4},{7,5},{0,6},{1,7},{10,8},{11,9},{12,... | collective-permute-start | bytes 1179656 | tf_op jit(solution)/shard_map/ppermute | solution.py:414
  49.0 17.3 %grad_in.1 = (f32[5,1536,512]{2,1,0:T(8,128)}, f32[5,1536,512]{2,1,0:T(8,128)}) custom-call(bf16[5,192,1536]{2,1,0:T(8,128)(2,1)} %get-tuple-element.21.x_ref, bf16[5,192,512]{2,1,0:T(8,128)(2,1)} %get-tuple-element.22.da_ref, bf16[5,192,512]{2,1,0:T(8,128)(2,1)} %get-tuple-element.23.db_ref), custom_call_target="tpu_custom_call" | custom-call | flops 3019898880 | bytes 31457280 | tf_op jit(solution)/shard_map/grad_in/pallas_call | solution.py:367
  66.4 0.0 collective-permute-done
  66.4 0.0 collective-permute-done.1
  66.4 0.0 copy-done.2
  66.4 0.7 collective-permute-start.3
  67.1 0.0 copy-done.1
  67.2 1.5 %collective-permute-start.2 = (f32[32,1536]{1,0:T(8,128)S(1)}, f32[32,1536]{1,0:T(8,128)S(1)}, u32[]{:S(2)}, u32[]{:S(2)}) collective-permute-start(f32[32,1536]{1,0:T(8,128)S(1)} %slice_add_fusion.1), channel_id=1, source_target_pairs={{0,2},{1,3},{2,4},{3,5},{4,6},{5,7},{6,0},{7,1},{8,10},{9,11},{10,... | collective-permute-start | bytes 589832 | tf_op jit(solution)/shard_map/ppermute | solution.py:417
  68.6 0.0 copy-start
  68.6 11.5 %grad_out.1 = f32[5,512,1536]{2,1,0:T(8,128)} custom-call(bf16[5,192,512]{2,1,0:T(8,128)(2,1)} %get-tuple-element.33.h_ref, bf16[5,192,1536]{2,1,0:T(8,128)(2,1)} %get-tuple-element.34.dz_ref), custom_call_target="tpu_custom_call" | custom-call | flops 1509949440 | bytes 15728640 | tf_op jit(solution)/shard_map/grad_out/pallas_call | solution.py:385
  80.1 0.0 collective-permute-done.3
  80.1 0.0 collective-permute-done.2
  80.1 0.0 copy-done
  80.1 0.1 add_convert_fusion.1
  80.2 0.7 pad_maximum_fusion
  (2 shorter events, 0.0 us)
Async XLA Ops:
  45.7 20.7 %copy-start.2 = (f32[32,1536]{1,0:T(8,128)S(1)}, f32[32,1536]{1,0:T(8,128)}, u32[]{:S(2)}) copy-start(f32[32,1536]{1,0:T(8,128)} %get-tuple-element.31) | copy-start | bytes 589828
  45.7 21.5 %copy-start.1 = (f32[32,1536]{1,0:T(8,128)S(1)}, f32[32,1536]{1,0:T(8,128)}, u32[]{:S(2)}) copy-start(f32[32,1536]{1,0:T(8,128)} %get-tuple-element.29) | copy-start | bytes 589828
  45.7 20.7 %collective-permute-start = (f32[64,1536]{1,0:T(8,128)}, f32[64,1536]{1,0:T(8,128)S(1)}, u32[]{:S(2)}, u32[]{:S(2)}) collective-permute-start(f32[64,1536]{1,0:T(8,128)} %get-tuple-element.26), channel_id=1, source_target_pairs={{0,2},{1,3},{2,4},{3,5},{4,6},{5,7},{6,0},{7,1},{8,10},{9,11},{10,... | collective-permute-start | bytes 1179656 | tf_op jit(solution)/shard_map/ppermute | solution.py:413
  46.4 20.0 %collective-permute-start.1 = (f32[64,1536]{1,0:T(8,128)}, f32[64,1536]{1,0:T(8,128)S(1)}, u32[]{:S(2)}, u32[]{:S(2)}) collective-permute-start(f32[64,1536]{1,0:T(8,128)} %get-tuple-element.27), channel_id=1, source_target_pairs={{2,0},{3,1},{4,2},{5,3},{6,4},{7,5},{0,6},{1,7},{10,8},{11,9},{12,... | collective-permute-start | bytes 1179656 | tf_op jit(solution)/shard_map/ppermute | solution.py:414
  66.4 13.7 %collective-permute-start.3 = (f32[32,1536]{1,0:T(8,128)S(1)}, f32[32,1536]{1,0:T(8,128)S(1)}, u32[]{:S(2)}, u32[]{:S(2)}) collective-permute-start(f32[32,1536]{1,0:T(8,128)S(1)} %slice_add_fusion), channel_id=1, source_target_pairs={{2,0},{3,1},{4,2},{5,3},{6,4},{7,5},{0,6},{1,7},{10,8},{11,9},{12,... | collective-permute-start | bytes 589832 | tf_op jit(solution)/shard_map/ppermute | solution.py:418
  67.2 12.9 %collective-permute-start.2 = (f32[32,1536]{1,0:T(8,128)S(1)}, f32[32,1536]{1,0:T(8,128)S(1)}, u32[]{:S(2)}, u32[]{:S(2)}) collective-permute-start(f32[32,1536]{1,0:T(8,128)S(1)} %slice_add_fusion.1), channel_id=1, source_target_pairs={{0,2},{1,3},{2,4},{3,5},{4,6},{5,7},{6,0},{7,1},{8,10},{9,11},{10,... | collective-permute-start | bytes 589832 | tf_op jit(solution)/shard_map/ppermute | solution.py:417
  68.6 11.5 %copy-start = (f32[64,1536]{1,0:T(8,128)S(1)}, f32[64,1536]{1,0:T(8,128)}, u32[]{:S(2)}) copy-start(f32[64,1536]{1,0:T(8,128)} %get-tuple-element.20) | copy-start | bytes 1179652

commit v2 on v1

v2 whole, which is shorter than its diff:
```python
import functools

import jax
import jax.numpy as jnp
from jax import lax
from jax.experimental import pallas as pl
from jax.experimental.pallas import tpu as pltpu
from jax.sharding import PartitionSpec as P

F32 = jnp.float32
BF16 = jnp.bfloat16
NT = (((1,), (1,)), ((), ()))
TN = (((0,), (0,)), ((), ()))
DY_Q = 3
DX_Q = 3
KEY_STRIDE = 256
N_COPIES = 36
OUT_TYPE = pltpu.VMEM


def slot_capacity(tok_dev, top_k, n_exp):
    return ((3 * tok_dev * top_k) // (2 * n_exp) + 7) // 8 * 8


def exchange_kernel(
    n_dev, cap,
    x_hbm, dy_hbm, ids_hbm, slot_hbm, gate_hbm, w1_hbm, w3_hbm, w2_hbm,
    xb, dz, hh, da, db, r1, l1, ra, lb, own,
    xg, dyg, ids, slots, gates_v, mt, w1, w3, w2, qq, uu, bb, dh, dxq,
    pm, pt, gm, part, sibr,
    loc_sem, w_sem, send, recv,
):
    n_exp = w1_hbm.shape[0]
    tok, d = x_hbm.shape
    half = tok // 2
    n_chip = n_dev // 2
    rc_rows = 2 * cap
    used = n_exp * rc_rows
    me = lax.axis_index("ep")
    chip, core = me // 2, lax.rem(me, 2)
    right = lax.rem(chip + 1, n_chip) * 2 + core
    left = lax.rem(chip + n_chip - 1, n_chip) * 2 + core
    sib = chip * 2 + 1 - core

    counter = [0]

    def remote(src, dst, dev):
        i = counter[0]
        counter[0] += 1
        return pltpu.make_async_remote_copy(
            src_ref=src, dst_ref=dst, send_sem=send.at[i], recv_sem=recv.at[i],
            device_id={"ep": dev}, device_id_type=pl.DeviceIdType.MESH)

    started = []

    def go(copy):
        copy.start()
        started.append(copy)
        return copy

    barrier = pltpu.get_barrier_semaphore()
    for dev in (right, left, sib):
        pl.semaphore_signal(barrier, inc=1, device_id={"ep": dev}, device_id_type=pl.DeviceIdType.MESH)

    loc = [
        pltpu.make_async_copy(src, dst, loc_sem.at[i])
        for i, (src, dst) in enumerate((
            (ids_hbm, ids), (slot_hbm, slots), (gate_hbm, gates_v),
            (x_hbm, xg.at[0, 0]), (dy_hbm, dyg.at[0, 0])))
    ]
    for c in loc:
        c.start()
    wcopies = {}
    for k, (src, dst) in enumerate(((w1_hbm, w1), (w3_hbm, w3), (w2_hbm, w2))):
        for e in range(n_exp):
            wcopies[k, e] = pltpu.make_async_copy(src.at[e], dst.at[e], w_sem.at[k * n_exp + e])

    with jax.named_scope("head_keys"):
        for c in loc[:3]:
            c.wait()
        expert, slot = ids[...].astype(F32), slots[...].astype(F32)
        owner = jnp.floor((expert + 0.5) / float(n_exp))
        keys = owner * float(KEY_STRIDE) + (expert - owner * n_exp) * float(rc_rows) + slot
        keys = jnp.where(slot >= 0.0, keys, -1000.0)
        for i in range(2):
            mt[0, 0, :8, i * tok:(i + 1) * tok] = keys
            mt[0, 0, 8:, i * tok:(i + 1) * tok] = gates_v[...]

    with jax.named_scope("head_barrier"):
        pl.semaphore_wait(barrier, 3)

    rows_i = lax.broadcasted_iota(jnp.int32, (KEY_STRIDE, 2 * tok), 0)
    lane_i = lax.broadcasted_iota(jnp.int32, (16, 2 * tok), 1)
    row_key = (rows_i + me * KEY_STRIDE).astype(F32)

    def build(s):
        m0, m1 = mt[s, 0], mt[s, 1]
        first = lane_i < tok
        keys = jnp.where(first, m0, m1 + float(cap))
        gates = jnp.where(first, m0, m1)
        ones = jnp.zeros((KEY_STRIDE, 2 * tok), F32)
        gmat = jnp.zeros((KEY_STRIDE, 2 * tok), F32)
        for j in range(8):
            hit = row_key == keys[j:j + 1, :]
            ones = jnp.where(hit, 1.0, ones)
            gmat = jnp.where(hit, gates[8 + j:9 + j, :], gmat)
        pm[s] = ones.astype(BF16)
        pt[s] = jnp.transpose(ones).astype(BF16)
        gm[s] = jnp.sum(gmat, axis=1, keepdims=True)

    def gather_x(s):
        src = xg[s].reshape(2 * tok, d)
        rows = jnp.dot(pm[s, :used, :], src, preferred_element_type=F32).astype(BF16)
        for e in range(n_exp):
            xb[e, s * rc_rows:(s + 1) * rc_rows, :] = rows[e * rc_rows:(e + 1) * rc_rows, :]

    def gather_dy(s, c):
        src = dyg[s, :, :, c].reshape(2 * tok, c.stop - c.start)
        rows = jnp.dot(pm[s, :used, :], src, preferred_element_type=F32)
        rows = (rows * gm[s, :used, :]).astype(BF16)
        for e in range(n_exp):
            dz[e, s * rc_rows:(s + 1) * rc_rows, c] = rows[e * rc_rows:(e + 1) * rc_rows, :]

    def up(e):
        wcopies[0, e].wait()
        wcopies[1, e].wait()
        x = xb[e]
        a16 = jnp.dot(x, w1[e], preferred_element_type=F32).astype(BF16)
        b16 = jnp.dot(x, w3[e], preferred_element_type=F32).astype(BF16)
        a = a16.astype(F32)
        b = b16.astype(F32)
        sg = jax.nn.sigmoid(a)
        silu = a * sg
        hh[e] = (silu * b).astype(BF16)
        uu[e] = silu
        qq[e] = sg * (1.0 + a * (1.0 - sg))
        bb[e] = b16

    lo, hi = pl.ds(0, half), pl.ds(half, half)
    qd = d // DY_Q
    dcol = [slice(q * qd, (q + 1) * qd) for q in range(DY_Q)]
    full = slice(0, d)

    def far_cols(q):
        return pl.ds(q * qd, qd)

    m_r = go(remote(mt.at[0, 0], mt.at[3, 0], right))
    m_l = go(remote(mt.at[0, 0], mt.at[1, 0], left))
    m_s = go(remote(mt.at[0, 0], mt.at[0, 1], sib))
    loc[3].wait()
    xa_r = go(remote(xg.at[0, 0, lo], xg.at[3, 0, lo], right))
    xb_l = go(remote(xg.at[0, 0, hi], xg.at[1, 0, hi], left))
    xb_r = go(remote(xg.at[0, 0, hi], xg.at[3, 0, hi], right))
    xa_l = go(remote(xg.at[0, 0, lo], xg.at[1, 0, lo], left))
    x_s = go(remote(xg.at[0, 0], xg.at[0, 1], sib))
    loc[4].wait()
    y_s = go(remote(dyg.at[0, 0], dyg.at[0, 1], sib))
    for e in range(n_exp):
        wcopies[0, e].start()
        wcopies[1, e].start()
    for e in range(n_exp):
        wcopies[2, e].start()
    with jax.named_scope("own_rows"):
        m_s.wait_recv()
        build(0)
        m_r.wait_recv()
        m_rr = go(remote(mt.at[3, 0], mt.at[2, 0], right))
        m_s3 = go(remote(mt.at[3, 0], mt.at[3, 1], sib))
        m_l.wait_recv()
        m_s1 = go(remote(mt.at[1, 0], mt.at[1, 1], sib))
        x_s.wait_recv()
        gather_x(0)
    with jax.named_scope("x_relay"):
        xa_r.wait_recv()
        xa_rr = go(remote(xg.at[3, 0, lo], xg.at[2, 0, lo], right))
        xb_l.wait_recv()
        xb_ll = go(remote(xg.at[1, 0, hi], xg.at[2, 0, hi], left))
        ya_r = go(remote(dyg.at[0, 0, lo], dyg.at[3, 0, lo], right))
        yb_l = go(remote(dyg.at[0, 0, hi], dyg.at[1, 0, hi], left))
        yb_r = go(remote(dyg.at[0, 0, hi], dyg.at[3, 0, hi], right))
        ya_l = go(remote(dyg.at[0, 0, lo], dyg.at[1, 0, lo], left))
    with jax.named_scope("build31"):
        m_s3.wait_recv()
        build(3)
        m_s1.wait_recv()
        build(1)
    with jax.named_scope("x_near"):
        xb_r.wait_recv()
        x_s3 = go(remote(xg.at[3, 0], xg.at[3, 1], sib))
        xa_l.wait_recv()
        x_s1 = go(remote(xg.at[1, 0], xg.at[1, 1], sib))
        m_rr.wait_recv()
        m_s2 = go(remote(mt.at[2, 0], mt.at[2, 1], sib))
        y_s.wait_recv()
        gather_dy(0, full)
        x_s3.wait_recv()
        gather_x(3)
        x_s1.wait_recv()
        gather_x(1)
    with jax.named_scope("x_far"):
        m_s2.wait_recv()
        build(2)
        xa_rr.wait_recv()
        xb_ll.wait_recv()
        x_s2 = go(remote(xg.at[2, 0], xg.at[2, 1], sib))
        x_s2.wait_recv()
        gather_x(2)
    with jax.named_scope("up0"):
        up(0)
    with jax.named_scope("y_relay"):
        ya_r.wait_recv()
        yb_l.wait_recv()
        yfar = []
        for q in range(DY_Q):
            c = far_cols(q)
            yfar.append((go(remote(dyg.at[3, 0, lo, c], dyg.at[2, 0, lo, c], right)),
                         go(remote(dyg.at[1, 0, hi, c], dyg.at[2, 0, hi, c], left))))
    with jax.named_scope("up12"):
        up(1)
        up(2)
    with jax.named_scope("y_near_fwd"):
        yb_r.wait_recv()
        y_s3 = go(remote(dyg.at[3, 0], dyg.at[3, 1], sib))
        ya_l.wait_recv()
        y_s1 = go(remote(dyg.at[1, 0], dyg.at[1, 1], sib))
    with jax.named_scope("up34"):
        for e in range(3, n_exp):
            up(e)

    y_s2 = []

    def y_far_fwd(q):
        c = far_cols(q)
        for copy in yfar[q]:
            copy.wait_recv()
        y_s2.append(go(remote(dyg.at[2, 0, :, c], dyg.at[2, 1, :, c], sib)))

    with jax.named_scope("y_near"):
        y_far_fwd(0)
        y_s3.wait_recv()
        gather_dy(3, full)
        y_s1.wait_recv()
        gather_dy(1, full)

    def down(e, q):
        c = dcol[q]
        if q == 0:
            wcopies[2, e].wait()
        val = lax.dot_general(dz[e, :, c], w2[e, :, c], NT, preferred_element_type=F32)
        if q > 0:
            val = val + dh[e]
        if q < DY_Q - 1:
            dh[e] = val
        else:
            da[e] = (val * bb[e].astype(F32) * qq[e]).astype(BF16)
            db[e] = (val * uu[e]).astype(BF16)

    for q in range(DY_Q):
        with jax.named_scope(f"y_far{q}"):
            if q + 1 < DY_Q:
                y_far_fwd(q + 1)
            y_s2[q].wait_recv()
            gather_dy(2, dcol[q])
        with jax.named_scope(f"down{q}"):
            for e in range(n_exp):
                down(e, q)

    qx = d // DX_Q
    sib_copies = []

    def dx_block(q):
        c = slice(q * qx, (q + 1) * qx)
        for e in range(n_exp):
            v = lax.dot_general(da[e], w1[e, c, :], NT, preferred_element_type=F32)
            v = v + lax.dot_general(db[e], w3[e, c, :], NT, preferred_element_type=F32)
            dxq[e] = v.astype(BF16)
        for s in range(n_chip):
            rows = dxq[:, s * rc_rows:(s + 1) * rc_rows, :].reshape(used, qx)
            part[q, s] = jnp.dot(pt[s, :, :used], rows, preferred_element_type=F32).reshape(2, tok, qx)
        sib_copies.append(go(remote(part.at[q, :, 1], sibr.at[q], sib)))

    def finish(q):
        c = slice(q * qx, (q + 1) * qx)
        sib_copies[q].wait_recv()

        def total(s, rs):
            return part[q, s, 0, rs] + sibr[q, s, rs]

        a, b = slice(0, half), slice(half, tok)
        r1[a, c] = total(2, a)
        r1[b, c] = total(1, b)
        l1[a, c] = total(3, a)
        l1[b, c] = total(2, b)
        ra[:, c] = total(1, a)
        lb[:, c] = total(3, b)
        own[:, c] = part[q, 0, 0] + sibr[q, 0]

    for q in range(DX_Q):
        with jax.named_scope(f"dx{q}"):
            dx_block(q)
        if q > 0:
            with jax.named_scope(f"finish{q - 1}"):
                finish(q - 1)
    with jax.named_scope(f"finish{DX_Q - 1}"):
        finish(DX_Q - 1)

    with jax.named_scope("send_wait"):
        for c in started:
            c.wait_send()
    assert counter[0] == N_COPIES


def run_exchange(x, dy, ids, slots, gates, w1, w3, w2, n_dev, cap):
    n_exp, d, f = w1.shape
    tok = x.shape[0]
    half = tok // 2
    n_chip = n_dev // 2
    rows = n_dev * cap
    used = n_exp * 2 * cap
    qx = d // DX_Q
    any_spec = pl.BlockSpec(memory_space=pl.ANY)
    vmem_spec = pl.BlockSpec(memory_space=pltpu.VMEM)
    sds = OUT_TYPE
    outs = (
        sds((n_exp, rows, d), BF16), sds((n_exp, rows, d), BF16),
        sds((n_exp, rows, f), BF16), sds((n_exp, rows, f), BF16), sds((n_exp, rows, f), BF16),
        sds((tok, d), F32), sds((tok, d), F32), sds((half, d), F32), sds((half, d), F32), sds((tok, d), F32),
    )
    scratch = [
        pltpu.VMEM((n_chip, 2, tok, d), BF16),
        pltpu.VMEM((n_chip, 2, tok, d), BF16),
        pltpu.VMEM(ids.shape, jnp.int32),
        pltpu.VMEM(ids.shape, jnp.int32),
        pltpu.VMEM(ids.shape, F32),
        pltpu.VMEM((n_chip, 2, 16, 2 * tok), F32),
        pltpu.VMEM((n_exp, d, f), BF16),
        pltpu.VMEM((n_exp, d, f), BF16),
        pltpu.VMEM((n_exp, f, d), BF16),
        pltpu.VMEM((n_exp, rows, f), F32),
        pltpu.VMEM((n_exp, rows, f), F32),
        pltpu.VMEM((n_exp, rows, f), BF16),
        pltpu.VMEM((n_exp, rows, f), F32),
        pltpu.VMEM((n_exp, rows, qx), BF16),
        pltpu.VMEM((n_chip, KEY_STRIDE, 2 * tok), BF16),
        pltpu.VMEM((n_chip, 2 * tok, KEY_STRIDE), BF16),
        pltpu.VMEM((n_chip, KEY_STRIDE, 1), F32),
        pltpu.VMEM((DX_Q, n_chip, 2, tok, qx), F32),
        pltpu.VMEM((DX_Q, n_chip, tok, qx), F32),
        pltpu.SemaphoreType.DMA((5,)),
        pltpu.SemaphoreType.DMA((3 * n_exp,)),
        pltpu.SemaphoreType.DMA((N_COPIES,)),
        pltpu.SemaphoreType.DMA((N_COPIES,)),
    ]
    return pl.pallas_call(
        functools.partial(exchange_kernel, n_dev, cap),
        out_shape=outs,
        in_specs=[any_spec] * 8,
        out_specs=(vmem_spec,) * len(outs),
        scratch_shapes=scratch,
        compiler_params=pltpu.CompilerParams(
            collective_id=0, has_side_effects=True, vmem_limit_bytes=54_000_000),
        name="exchange",
    )(x, dy, ids, slots, gates, w1, w3, w2)


def grad_in_kernel(blk, x, da, db, g1_hbm, g3_hbm, g1, g3, sem):
    n_exp, rows, d = x.shape
    n_blk = d // blk

    def store(e, k):
        rs = pl.ds(k * blk, blk)
        return [pltpu.make_async_copy(src.at[e, rs], dst.at[e, rs], sem.at[o, e, k])
                for o, (src, dst) in enumerate(((g1, g1_hbm), (g3, g3_hbm)))]

    def step(e, carry):
        for k in range(n_blk):
            rs = slice(k * blk, (k + 1) * blk)
            xt = x[e, :, rs]
            g1[e, rs, :] = lax.dot_general(xt, da[e], TN, preferred_element_type=F32)
            g3[e, rs, :] = lax.dot_general(xt, db[e], TN, preferred_element_type=F32)
            for c in store(e, k):
                c.start()
        return carry

    lax.fori_loop(0, n_exp, step, 0)

    def drain(e, carry):
        for k in range(n_blk):
            for c in store(e, k):
                c.wait()
        return carry

    lax.fori_loop(0, n_exp, drain, 0)


def grad_in(xb, da, db, blk=512):
    n_exp, rows, d = xb.shape
    f = da.shape[2]
    any_spec = pl.BlockSpec(memory_space=pl.ANY)
    out = jax.ShapeDtypeStruct((n_exp, d, f), F32)
    return pl.pallas_call(
        functools.partial(grad_in_kernel, blk),
        out_shape=(out, out),
        in_specs=[pl.BlockSpec(memory_space=pltpu.VMEM)] * 3,
        out_specs=(any_spec, any_spec),
        scratch_shapes=[
            pltpu.VMEM(out.shape, F32), pltpu.VMEM(out.shape, F32),
            pltpu.SemaphoreType.DMA((2, n_exp, d // blk))],
        compiler_params=pltpu.CompilerParams(vmem_limit_bytes=40_000_000),
        cost_estimate=pl.CostEstimate(flops=4 * n_exp * rows * d * f, bytes_accessed=8 * n_exp * d * f, transcendentals=0),
        name="grad_in",
    )(xb, da, db)


def grad_out_kernel(blk, h, dz, g_hbm, g, sem):
    n_exp, rows, f = h.shape
    n_blk = f // blk

    def store(e, k):
        rs = pl.ds(k * blk, blk)
        return pltpu.make_async_copy(g.at[e, rs], g_hbm.at[e, rs], sem.at[e, k])

    def step(e, carry):
        for k in range(n_blk):
            rs = slice(k * blk, (k + 1) * blk)
            g[e, rs, :] = lax.dot_general(h[e, :, rs], dz[e], TN, preferred_element_type=F32)
            store(e, k).start()
        return carry

    lax.fori_loop(0, n_exp, step, 0)

    def drain(e, carry):
        for k in range(n_blk):
            store(e, k).wait()
        return carry

    lax.fori_loop(0, n_exp, drain, 0)


def grad_out(h, dz, blk=256):
    n_exp, rows, f = h.shape
    d = dz.shape[2]
    out = jax.ShapeDtypeStruct((n_exp, f, d), F32)
    return pl.pallas_call(
        functools.partial(grad_out_kernel, blk),
        out_shape=out,
        in_specs=[pl.BlockSpec(memory_space=pltpu.VMEM)] * 2,
        out_specs=pl.BlockSpec(memory_space=pl.ANY),
        scratch_shapes=[pltpu.VMEM(out.shape, F32), pltpu.SemaphoreType.DMA((n_exp, f // blk))],
        compiler_params=pltpu.CompilerParams(vmem_limit_bytes=24_000_000),
        cost_estimate=pl.CostEstimate(flops=2 * n_exp * rows * d * f, bytes_accessed=4 * n_exp * d * f, transcendentals=0),
        name="grad_out",
    )(h, dz)


def combine_kernel(own, r1, l1, r2, l2, out):
    half = r2.shape[0]
    out[:half, :] = (own[:half, :] + l1[:half, :] + r2[...]).astype(BF16)
    out[half:, :] = (own[half:, :] + r1[half:, :] + l2[...]).astype(BF16)


def combine(own, r1, l1, r2, l2):
    return pl.pallas_call(
        combine_kernel,
        out_shape=jax.ShapeDtypeStruct(own.shape, BF16),
        in_specs=[pl.BlockSpec(memory_space=pltpu.VMEM)] * 5,
        out_specs=pl.BlockSpec(memory_space=pltpu.VMEM),
        compiler_params=pltpu.CompilerParams(vmem_limit_bytes=8_000_000),
        name="combine",
    )(own, r1, l1, r2, l2)


def solution(mesh):
    n_dev = mesh.shape["ep"]
    n_chip = n_dev // 2

    def local_step(x_loc, dy_loc, ids_loc, gate_loc, slot_loc, w_gate, w_down, w_up):
        tok, top_k = ids_loc.shape
        n_local = w_gate.shape[0]
        cap = slot_capacity(tok, top_k, n_local * n_dev)
        half = tok // 2
        xb, dz, h, da, db, r1, l1, ra, lb, own = run_exchange(
            x_loc, dy_loc, ids_loc.T, slot_loc.T, gate_loc.T, w_gate, w_up, w_down, n_dev, cap)
        to_right = [(c * 2 + k, (c + 1) % n_chip * 2 + k) for c in range(n_chip) for k in range(2)]
        to_left = [(b, a) for a, b in to_right]
        r1 = lax.ppermute(r1, "ep", to_right)
        l1 = lax.ppermute(l1, "ep", to_left)
        g_gate, g_up = grad_in(xb, da, db)
        g_gate, g_up, r1, l1 = lax.optimization_barrier((g_gate, g_up, r1, l1))
        r2 = lax.ppermute(ra + r1[:half], "ep", to_right)
        l2 = lax.ppermute(lb + l1[half:], "ep", to_left)
        g_down = grad_out(h, dz)
        dx = combine(own, r1, l1, r2, l2)
        return dx, g_gate, g_down, g_up

    tok_spec = P(("dp", "ep"), None)
    w_spec = P("ep", None, None)
    grad_spec = P(("dp", "ep"), None, None)
    return jax.shard_map(
        local_step, mesh=mesh,
        in_specs=(tok_spec,) * 5 + (w_spec,) * 3,
        out_specs=(tok_spec, grad_spec, grad_spec, grad_spec),
        check_vma=False)
```

time: 81.6 us -> 56.9 us (0.70)
  Pallas kernels: 71.7 us -> 50.3 us
  other arithmetic: 2.96 us -> 0.06 us
    pallas_call x2 -> x3, Pallas kernels: 28.8 us -> 17.6 us  [the longest x1 10.8 us: grad_in(): pl.pallas_call(functools.partial(grad_in_kernel, blk), out_shape=(out, ou...]
    pallas_call x1, Pallas kernels: 42.9 us -> 32.7 us  [run_exchange(): pl.pallas_call(functools.partial(exchange_kernel, n_dev, cap), out_shape=...]
    concatenate x2 -> x0, other arithmetic: 2.13 us -> none  [the longest x1 1.44 us: local_step(): meta = jnp.concatenate([meta, meta], axis=1)]
  transfers between devices with their start and end apart: 4 -> 4, of which waited for: 0 -> 1; matrix products, arithmetic and copies ran while one was open for 0% -> 0% of each run, Pallas kernels for 36% -> 30%
where the time goes in v2:
time: 56.9 us; the launch traced here: 56.8 us
  Pallas kernels  50.3 us (88%)
  starting transfers between devices  5.5 us (10%)
  between operations  0.69 us (1%)
    pallas_call x1, Pallas kernels, run_exchange(): pl.pallas_call(functools.partial(exchange_kernel, n_dev, cap), out_shape=...  32.7 us
    pallas_call x1, Pallas kernels, grad_in(): pl.pallas_call(functools.partial(grad_in_kernel, blk), out_shape=(out, ou...  10.8 us
    pallas_call x1, Pallas kernels, grad_out(): pl.pallas_call(functools.partial(grad_out_kernel, blk), out_shape=out, in...  6.01 us
    ppermute x1, starting transfers between devices, local_step(): l1 = lax.ppermute(l1, 'ep', to_left)  2.81 us
    ppermute x1, starting transfers between devices, local_step(): l2 = lax.ppermute(lb + l1[half:], 'ep', to_left)  1.47 us
  transfers between devices with their start and end apart: 4, of which 1 were waited for; matrix products, arithmetic and copies ran while one was open for 0% of the time, Pallas kernels for 30%

profile of v2, /device:TPU:112, one launch (start us, length us, event | category | flops | bytes accessed | tf_op | source)
XLA Modules:
  0.0 56.8 jit_solution(10323428519868209134)
XLA Ops:
  0.6 32.7 %exchange.1 = (bf16[5,192,1536]{2,1,0:T(8,128)(2,1)S(1)}, bf16[5,192,1536]{2,1,0:T(8,128)(2,1)S(1)}, bf16[5,192,512]{2,1,0:T(8,128)(2,1)S(1)}, bf16[5,192,512]{2...) custom-call(bf16[64,1536]{1,0:T(8,128)(2,1)} %x_hbm.1, ...), custom_call_target="tpu_custom_call" | custom-call | tf_op jit(solution)/shard_map/exchange/pallas_call | solution.py:354
  33.4 0.5 collective-permute-start
  33.9 2.8 %collective-permute-start.1 = (f32[64,1536]{1,0:T(8,128)S(1)}, f32[64,1536]{1,0:T(8,128)S(1)}, u32[]{:S(2)}, u32[]{:S(2)}) collective-permute-start(f32[64,1536]{1,0:T(8,128)S(1)} %get-tuple-element.27), channel_id=1, source_target_pairs={{2,0},{3,1},{4,2},{5,3},{6,4},{7,5},{0,6},{1,7},{10,8},{11,9},{12,... | collective-permute-start | bytes 1179656 | tf_op jit(solution)/shard_map/ppermute | solution.py:487
  36.7 10.8 %grad_in.1 = (f32[5,1536,512]{2,1,0:T(8,128)}, f32[5,1536,512]{2,1,0:T(8,128)}) custom-call(bf16[5,192,1536]{2,1,0:T(8,128)(2,1)S(1)} %get-tuple-element.21.x, bf16[5,192,512]{2,1,0:T(8,128)(2,1)S(1)} %get-tuple-element.22.da, bf16[5,192,512]{2,1,0:T(8,128)(2,1)S(1)} %get-tuple-element.23.db), custom_call_target="tpu_custom_call" | custom-call | flops 3019898880 | bytes 31457280 | tf_op jit(solution)/shard_map/grad_in/pallas_call | solution.py:401
  47.5 0.0 collective-permute-done.r1
  47.5 0.0 collective-permute-done.1.l1
  47.6 1.5 %collective-permute-start.3 = (f32[32,1536]{1,0:T(8,128)S(1)}, f32[32,1536]{1,0:T(8,128)S(1)}, u32[]{:S(2)}, u32[]{:S(2)}) collective-permute-start(f32[32,1536]{1,0:T(8,128)S(1)} %slice_add_fusion), channel_id=1, source_target_pairs={{2,0},{3,1},{4,2},{5,3},{6,4},{7,5},{0,6},{1,7},{10,8},{11,9},{12,... | collective-permute-start | bytes 589832 | tf_op jit(solution)/shard_map/ppermute | solution.py:491
  49.1 0.7 %collective-permute-start.2 = (f32[32,1536]{1,0:T(8,128)S(1)}, f32[32,1536]{1,0:T(8,128)S(1)}, u32[]{:S(2)}, u32[]{:S(2)}) collective-permute-start(f32[32,1536]{1,0:T(8,128)S(1)} %slice_add_fusion.1), channel_id=1, source_target_pairs={{0,2},{1,3},{2,4},{3,5},{4,6},{5,7},{6,0},{7,1},{8,10},{9,11},{10,... | collective-permute-start | bytes 589832 | tf_op jit(solution)/shard_map/ppermute | solution.py:490
  49.8 6.0 %grad_out.1 = f32[5,512,1536]{2,1,0:T(8,128)} custom-call(bf16[5,192,512]{2,1,0:T(8,128)(2,1)S(1)} %get-tuple-element.33.h, bf16[5,192,1536]{2,1,0:T(8,128)(2,1)S(1)} %get-tuple-element.34.dz), custom_call_target="tpu_custom_call" | custom-call | flops 1509949440 | bytes 15728640 | tf_op jit(solution)/shard_map/grad_out/pallas_call | solution.py:444
  55.8 0.0 collective-permute-done.3.l2
  55.8 0.3 collective-permute-done.2.r2
  56.1 0.7 %combine.1 = bf16[64,1536]{1,0:T(8,128)(2,1)} custom-call(f32[64,1536]{1,0:T(8,128)S(1)} %get-tuple-element.20.own, f32[64,1536]{1,0:T(8,128)S(1)} %collective-permute-done.r1, f32[64,1536]{1,0:T(8,128)S(1)} %collective-permute-done.1.l1, f32[32,1536]{1,0:T(8,128)S(1)} %collective-permute-done.2.r2, f32[32,1536]{1,0:T(8,128)S(1)} %collective-permute-done.3.l2), custom_call_target="tpu_custom_call" | custom-call | tf_op jit(solution)/shard_map/combine/pallas_call | solution.py:463
  (2 shorter events, 0.1 us)
Async XLA Ops:
  33.4 14.2 %collective-permute-start = (f32[64,1536]{1,0:T(8,128)S(1)}, f32[64,1536]{1,0:T(8,128)S(1)}, u32[]{:S(2)}, u32[]{:S(2)}) collective-permute-start(f32[64,1536]{1,0:T(8,128)S(1)} %get-tuple-element.26), channel_id=1, source_target_pairs={{0,2},{1,3},{2,4},{3,5},{4,6},{5,7},{6,0},{7,1},{8,10},{9,11},{10,... | collective-permute-start | bytes 1179656 | tf_op jit(solution)/shard_map/ppermute | solution.py:486
  33.9 13.7 %collective-permute-start.1 = (f32[64,1536]{1,0:T(8,128)S(1)}, f32[64,1536]{1,0:T(8,128)S(1)}, u32[]{:S(2)}, u32[]{:S(2)}) collective-permute-start(f32[64,1536]{1,0:T(8,128)S(1)} %get-tuple-element.27), channel_id=1, source_target_pairs={{2,0},{3,1},{4,2},{5,3},{6,4},{7,5},{0,6},{1,7},{10,8},{11,9},{12,... | collective-permute-start | bytes 1179656 | tf_op jit(solution)/shard_map/ppermute | solution.py:487
  47.6 8.2 %collective-permute-start.3 = (f32[32,1536]{1,0:T(8,128)S(1)}, f32[32,1536]{1,0:T(8,128)S(1)}, u32[]{:S(2)}, u32[]{:S(2)}) collective-permute-start(f32[32,1536]{1,0:T(8,128)S(1)} %slice_add_fusion), channel_id=1, source_target_pairs={{2,0},{3,1},{4,2},{5,3},{6,4},{7,5},{0,6},{1,7},{10,8},{11,9},{12,... | collective-permute-start | bytes 589832 | tf_op jit(solution)/shard_map/ppermute | solution.py:491
  49.1 7.0 %collective-permute-start.2 = (f32[32,1536]{1,0:T(8,128)S(1)}, f32[32,1536]{1,0:T(8,128)S(1)}, u32[]{:S(2)}, u32[]{:S(2)}) collective-permute-start(f32[32,1536]{1,0:T(8,128)S(1)} %slice_add_fusion.1), channel_id=1, source_target_pairs={{0,2},{1,3},{2,4},{3,5},{4,6},{5,7},{6,0},{7,1},{8,10},{9,11},{10,... | collective-permute-start | bytes 589832 | tf_op jit(solution)/shard_map/ppermute | solution.py:490

commit v3 on v2

--- a/solution.py
+++ b/solution.py
@@ -12,9 +12,9 @@
 NT = (((1,), (1,)), ((), ()))
 TN = (((0,), (0,)), ((), ()))
 DY_Q = 3
-DX_Q = 3
+DX_COLS = (512, 512, 256, 256)
 KEY_STRIDE = 256
-N_COPIES = 36
+N_COPIES = 45
 OUT_TYPE = pltpu.VMEM
 
 
@@ -25,9 +25,9 @@
 def exchange_kernel(
     n_dev, cap,
     x_hbm, dy_hbm, ids_hbm, slot_hbm, gate_hbm, w1_hbm, w3_hbm, w2_hbm,
-    xb, dz, hh, da, db, r1, l1, ra, lb, own,
+    xb, dz, hh, da, db, to_right, to_left, own,
     xg, dyg, ids, slots, gates_v, mt, w1, w3, w2, qq, uu, bb, dh, dxq,
-    pm, pt, gm, part, sibr,
+    pm, pt, gm, part, sibr, far_out, far_in,
     loc_sem, w_sem, send, recv,
 ):
     n_exp = w1_hbm.shape[0]
@@ -71,9 +71,10 @@
     for c in loc:
         c.start()
     wcopies = {}
-    for k, (src, dst) in enumerate(((w1_hbm, w1), (w3_hbm, w3), (w2_hbm, w2))):
+    for k, (src, dst) in enumerate(((w1_hbm, w1), (w3_hbm, w3))):
         for e in range(n_exp):
             wcopies[k, e] = pltpu.make_async_copy(src.at[e], dst.at[e], w_sem.at[k * n_exp + e])
+    w2copy = pltpu.make_async_copy(w2_hbm, w2, w_sem.at[2 * n_exp])
 
     with jax.named_scope("head_keys"):
         for c in loc[:3]:
@@ -158,8 +159,7 @@
     for e in range(n_exp):
         wcopies[0, e].start()
         wcopies[1, e].start()
-    for e in range(n_exp):
-        wcopies[2, e].start()
+    w2copy.start()
     with jax.named_scope("own_rows"):
         m_s.wait_recv()
         build(0)
@@ -244,8 +244,6 @@
 
     def down(e, q):
         c = dcol[q]
-        if q == 0:
-            wcopies[2, e].wait()
         val = lax.dot_general(dz[e, :, c], w2[e, :, c], NT, preferred_element_type=F32)
         if q > 0:
             val = val + dh[e]
@@ -255,6 +253,7 @@
             da[e] = (val * bb[e].astype(F32) * qq[e]).astype(BF16)
             db[e] = (val * uu[e]).astype(BF16)
 
+    w2copy.wait()
     for q in range(DY_Q):
         with jax.named_scope(f"y_far{q}"):
             if q + 1 < DY_Q:
@@ -265,45 +264,62 @@
             for e in range(n_exp):
                 down(e, q)
 
-    qx = d // DX_Q
-    sib_copies = []
+    starts = [sum(DX_COLS[:q]) for q in range(len(DX_COLS))]
+    sib_copies, far_copies = [], []
+
+    def cols(q):
+        return slice(starts[q], starts[q] + DX_COLS[q])
 
     def dx_block(q):
-        c = slice(q * qx, (q + 1) * qx)
+        c, w = cols(q), DX_COLS[q]
         for e in range(n_exp):
             v = lax.dot_general(da[e], w1[e, c, :], NT, preferred_element_type=F32)
             v = v + lax.dot_general(db[e], w3[e, c, :], NT, preferred_element_type=F32)
-            dxq[e] = v.astype(BF16)
+            dxq[e, :, :w] = v.astype(BF16)
         for s in range(n_chip):
-            rows = dxq[:, s * rc_rows:(s + 1) * rc_rows, :].reshape(used, qx)
-            part[q, s] = jnp.dot(pt[s, :, :used], rows, preferred_element_type=F32).reshape(2, tok, qx)
-        sib_copies.append(go(remote(part.at[q, :, 1], sibr.at[q], sib)))
+            rows = dxq[:, s * rc_rows:(s + 1) * rc_rows, :w].reshape(used, w)
+            part[s, :, :, c] = jnp.dot(pt[s, :, :used], rows, preferred_element_type=F32).reshape(2, tok, w)
+        cs = pl.ds(starts[q], w)
+        sib_copies.append(go(remote(part.at[:, 1, :, cs], sibr.at[:, :, cs], sib)))
+
+    def total(s, rs, c):
+        return part[s, 0, rs, c] + sibr[s, rs, c]
+
+    a_rows, b_rows, all_rows = slice(0, half), slice(half, tok), slice(0, tok)
 
     def finish(q):
-        c = slice(q * qx, (q + 1) * qx)
+        c = cols(q)
         sib_copies[q].wait_recv()
-
-        def total(s, rs):
-            return part[q, s, 0, rs] + sibr[q, s, rs]
-
-        a, b = slice(0, half), slice(half, tok)
-        r1[a, c] = total(2, a)
-        r1[b, c] = total(1, b)
-        l1[a, c] = total(3, a)
-        l1[b, c] = total(2, b)
-        ra[:, c] = total(1, a)
-        lb[:, c] = total(3, b)
-        own[:, c] = part[q, 0, 0] + sibr[q, 0]
-
-    for q in range(DX_Q):
+        far_out[:, c] = total(2, all_rows, c)
+        to_right[b_rows, c] = total(1, b_rows, c)
+        to_left[a_rows, c] = total(3, a_rows, c)
+        own[:, c] = total(0, all_rows, c)
+        cs = pl.ds(starts[q], DX_COLS[q])
+        far_copies.append((go(remote(far_out.at[lo, cs], far_in.at[lo, cs], right)),
+                           go(remote(far_out.at[hi, cs], far_in.at[hi, cs], left))))
+
+    def finish_far(q):
+        c = cols(q)
+        far_copies[q][0].wait_recv()
+        to_right[a_rows, c] = total(1, a_rows, c) + far_in[a_rows, c]
+        far_copies[q][1].wait_recv()
+        to_left[b_rows, c] = total(3, b_rows, c) + far_in[b_rows, c]
+
+    n_blocks = len(DX_COLS)
+    for q in range(n_blocks):
         with jax.named_scope(f"dx{q}"):
             dx_block(q)
-        if q > 0:
+        if q >= 1:
             with jax.named_scope(f"finish{q - 1}"):
                 finish(q - 1)
-    with jax.named_scope(f"finish{DX_Q - 1}"):
-        finish(DX_Q - 1)
-
+        if q >= 2:
+            with jax.named_scope(f"far{q - 2}"):
+                finish_far(q - 2)
+    with jax.named_scope("finish_last"):
+        finish(n_blocks - 1)
+    with jax.named_scope("far_last"):
+        finish_far(n_blocks - 2)
+        finish_far(n_blocks - 1)
     with jax.named_scope("send_wait"):
         for c in started:
             c.wait_send()
@@ -313,18 +329,15 @@
 def run_exchange(x, dy, ids, slots, gates, w1, w3, w2, n_dev, cap):
     n_exp, d, f = w1.shape
     tok = x.shape[0]
-    half = tok // 2
     n_chip = n_dev // 2
     rows = n_dev * cap
-    used = n_exp * 2 * cap
-    qx = d // DX_Q
     any_spec = pl.BlockSpec(memory_space=pl.ANY)
     vmem_spec = pl.BlockSpec(memory_space=pltpu.VMEM)
     sds = OUT_TYPE
     outs = (
         sds((n_exp, rows, d), BF16), sds((n_exp, rows, d), BF16),
         sds((n_exp, rows, f), BF16), sds((n_exp, rows, f), BF16), sds((n_exp, rows, f), BF16),
-        sds((tok, d), F32), sds((tok, d), F32), sds((half, d), F32), sds((half, d), F32), sds((tok, d), F32),
+        sds((tok, d), F32), sds((tok, d), F32), sds((tok, d), F32),
     )
     scratch = [
         pltpu.VMEM((n_chip, 2, tok, d), BF16),
@@ -340,14 +353,16 @@
         pltpu.VMEM((n_exp, rows, f), F32),
         pltpu.VMEM((n_exp, rows, f), BF16),
         pltpu.VMEM((n_exp, rows, f), F32),
-        pltpu.VMEM((n_exp, rows, qx), BF16),
+        pltpu.VMEM((n_exp, rows, max(DX_COLS)), BF16),
         pltpu.VMEM((n_chip, KEY_STRIDE, 2 * tok), BF16),
         pltpu.VMEM((n_chip, 2 * tok, KEY_STRIDE), BF16),
         pltpu.VMEM((n_chip, KEY_STRIDE, 1), F32),
-        pltpu.VMEM((DX_Q, n_chip, 2, tok, qx), F32),
-        pltpu.VMEM((DX_Q, n_chip, tok, qx), F32),
+        pltpu.VMEM((n_chip, 2, tok, d), F32),
+        pltpu.VMEM((n_chip, tok, d), F32),
+        pltpu.VMEM((tok, d), F32),
+        pltpu.VMEM((tok, d), F32),
         pltpu.SemaphoreType.DMA((5,)),
-        pltpu.SemaphoreType.DMA((3 * n_exp,)),
+        pltpu.SemaphoreType.DMA((2 * n_exp + 1,)),
         pltpu.SemaphoreType.DMA((N_COPIES,)),
         pltpu.SemaphoreType.DMA((N_COPIES,)),
     ]
@@ -363,111 +378,88 @@
     )(x, dy, ids, slots, gates, w1, w3, w2)
 
 
-def grad_in_kernel(blk, x, da, db, g1_hbm, g3_hbm, g1, g3, sem):
+def grads_kernel(in_blk, out_blk, x, dz, h, da, db, g1_hbm, g3_hbm, g2_hbm, g1, g3, g2, sem):
     n_exp, rows, d = x.shape
-    n_blk = d // blk
-
-    def store(e, k):
+    f = h.shape[2]
+    pieces = [((g1, g1_hbm), k, in_blk) for k in range(d // in_blk)]
+    pieces += [((g3, g3_hbm), k, in_blk) for k in range(d // in_blk)]
+    pieces += [((g2, g2_hbm), k, out_blk) for k in range(f // out_blk)]
+
+    n_in = d // in_blk
+    depth = g2.shape[0]
+
+    def store(e, i):
+        (src, dst), k, blk = pieces[i]
         rs = pl.ds(k * blk, blk)
-        return [pltpu.make_async_copy(src.at[e, rs], dst.at[e, rs], sem.at[o, e, k])
-                for o, (src, dst) in enumerate(((g1, g1_hbm), (g3, g3_hbm)))]
+        slot = lax.rem(e, depth) if i >= 2 * n_in else e
+        return pltpu.make_async_copy(src.at[slot, rs], dst.at[e, rs], sem.at[e, i])
 
     def step(e, carry):
-        for k in range(n_blk):
-            rs = slice(k * blk, (k + 1) * blk)
+        for k in range(n_in):
+            rs = slice(k * in_blk, (k + 1) * in_blk)
             xt = x[e, :, rs]
             g1[e, rs, :] = lax.dot_general(xt, da[e], TN, preferred_element_type=F32)
+            store(e, k).start()
             g3[e, rs, :] = lax.dot_general(xt, db[e], TN, preferred_element_type=F32)
-            for c in store(e, k):
-                c.start()
+            store(e, n_in + k).start()
+        @pl.when(e >= depth)
+        def _():
+            for k in range(f // out_blk):
+                store(e - depth, 2 * n_in + k).wait()
+
+        for k in range(f // out_blk):
+            rs = slice(k * out_blk, (k + 1) * out_blk)
+            g2[lax.rem(e, depth), rs, :] = lax.dot_general(h[e, :, rs], dz[e], TN, preferred_element_type=F32)
+            store(e, 2 * n_in + k).start()
         return carry
 
     lax.fori_loop(0, n_exp, step, 0)
 
     def drain(e, carry):
-        for k in range(n_blk):
-            for c in store(e, k):
-                c.wait()
+        for i in range(2 * n_in):
+            store(e, i).wait()
         return carry
 
     lax.fori_loop(0, n_exp, drain, 0)
-
-
-def grad_in(xb, da, db, blk=512):
+    for e in range(n_exp - depth, n_exp):
+        for k in range(f // out_blk):
+            store(e, 2 * n_in + k).wait()
+
+
+def weight_grads(xb, dz, h, da, db, in_blk=512, out_blk=256):
     n_exp, rows, d = xb.shape
     f = da.shape[2]
     any_spec = pl.BlockSpec(memory_space=pl.ANY)
-    out = jax.ShapeDtypeStruct((n_exp, d, f), F32)
+    g_in = jax.ShapeDtypeStruct((n_exp, d, f), F32)
+    g_out = jax.ShapeDtypeStruct((n_exp, f, d), F32)
+    n_pieces = 2 * (d // in_blk) + f // out_blk
     return pl.pallas_call(
-        functools.partial(grad_in_kernel, blk),
-        out_shape=(out, out),
-        in_specs=[pl.BlockSpec(memory_space=pltpu.VMEM)] * 3,
-        out_specs=(any_spec, any_spec),
+        functools.partial(grads_kernel, in_blk, out_blk),
+        out_shape=(g_in, g_in, g_out),
+        in_specs=[pl.BlockSpec(memory_space=pltpu.VMEM)] * 5,
+        out_specs=(any_spec,) * 3,
         scratch_shapes=[
-            pltpu.VMEM(out.shape, F32), pltpu.VMEM(out.shape, F32),
-            pltpu.SemaphoreType.DMA((2, n_exp, d // blk))],
-        compiler_params=pltpu.CompilerParams(vmem_limit_bytes=40_000_000),
-        cost_estimate=pl.CostEstimate(flops=4 * n_exp * rows * d * f, bytes_accessed=8 * n_exp * d * f, transcendentals=0),
-        name="grad_in",
-    )(xb, da, db)
-
-
-def grad_out_kernel(blk, h, dz, g_hbm, g, sem):
-    n_exp, rows, f = h.shape
-    n_blk = f // blk
-
-    def store(e, k):
-        rs = pl.ds(k * blk, blk)
-        return pltpu.make_async_copy(g.at[e, rs], g_hbm.at[e, rs], sem.at[e, k])
-
-    def step(e, carry):
-        for k in range(n_blk):
-            rs = slice(k * blk, (k + 1) * blk)
-            g[e, rs, :] = lax.dot_general(h[e, :, rs], dz[e], TN, preferred_element_type=F32)
-            store(e, k).start()
-        return carry
-
-    lax.fori_loop(0, n_exp, step, 0)
-
-    def drain(e, carry):
-        for k in range(n_blk):
-            store(e, k).wait()
-        return carry
-
-    lax.fori_loop(0, n_exp, drain, 0)
-
-
-def grad_out(h, dz, blk=256):
-    n_exp, rows, f = h.shape
-    d = dz.shape[2]
-    out = jax.ShapeDtypeStruct((n_exp, f, d), F32)
-    return pl.pallas_call(
-        functools.partial(grad_out_kernel, blk),
-        out_shape=out,
-        in_specs=[pl.BlockSpec(memory_space=pltpu.VMEM)] * 2,
-        out_specs=pl.BlockSpec(memory_space=pl.ANY),
-        scratch_shapes=[pltpu.VMEM(out.shape, F32), pltpu.SemaphoreType.DMA((n_exp, f // blk))],
-        compiler_params=pltpu.CompilerParams(vmem_limit_bytes=24_000_000),
-        cost_estimate=pl.CostEstimate(flops=2 * n_exp * rows * d * f, bytes_accessed=4 * n_exp * d * f, transcendentals=0),
-        name="grad_out",
-    )(h, dz)
-
-
-def combine_kernel(own, r1, l1, r2, l2, out):
-    half = r2.shape[0]
-    out[:half, :] = (own[:half, :] + l1[:half, :] + r2[...]).astype(BF16)
-    out[half:, :] = (own[half:, :] + r1[half:, :] + l2[...]).astype(BF16)
-
-
-def combine(own, r1, l1, r2, l2):
+            pltpu.VMEM(g_in.shape, F32), pltpu.VMEM(g_in.shape, F32), pltpu.VMEM((min(2, n_exp), f, d), F32),
+            pltpu.SemaphoreType.DMA((n_exp, n_pieces))],
+        compiler_params=pltpu.CompilerParams(vmem_limit_bytes=42_000_000),
+        cost_estimate=pl.CostEstimate(flops=6 * n_exp * rows * d * f, bytes_accessed=12 * n_exp * d * f, transcendentals=0),
+        name="weight_grads",
+    )(xb, dz, h, da, db)
+
+
+def combine_kernel(own, from_left, from_right, out):
+    out[...] = (own[...] + from_left[...] + from_right[...]).astype(BF16)
+
+
+def combine(own, from_left, from_right):
     return pl.pallas_call(
         combine_kernel,
         out_shape=jax.ShapeDtypeStruct(own.shape, BF16),
-        in_specs=[pl.BlockSpec(memory_space=pltpu.VMEM)] * 5,
+        in_specs=[pl.BlockSpec(memory_space=pltpu.VMEM)] * 3,
         out_specs=pl.BlockSpec(memory_space=pltpu.VMEM),
         compiler_params=pltpu.CompilerParams(vmem_limit_bytes=8_000_000),
         name="combine",
-    )(own, r1, l1, r2, l2)
+    )(own, from_left, from_right)
 
 
 def solution(mesh):
@@ -478,19 +470,14 @@
         tok, top_k = ids_loc.shape
         n_local = w_gate.shape[0]
         cap = slot_capacity(tok, top_k, n_local * n_dev)
-        half = tok // 2
-        xb, dz, h, da, db, r1, l1, ra, lb, own = run_exchange(
+        xb, dz, h, da, db, to_right, to_left, own = run_exchange(
             x_loc, dy_loc, ids_loc.T, slot_loc.T, gate_loc.T, w_gate, w_up, w_down, n_dev, cap)
-        to_right = [(c * 2 + k, (c + 1) % n_chip * 2 + k) for c in range(n_chip) for k in range(2)]
-        to_left = [(b, a) for a, b in to_right]
-        r1 = lax.ppermute(r1, "ep", to_right)
-        l1 = lax.ppermute(l1, "ep", to_left)
-        g_gate, g_up = grad_in(xb, da, db)
-        g_gate, g_up, r1, l1 = lax.optimization_barrier((g_gate, g_up, r1, l1))
-        r2 = lax.ppermute(ra + r1[:half], "ep", to_right)
-        l2 = lax.ppermute(lb + l1[half:], "ep", to_left)
-        g_down = grad_out(h, dz)
-        dx = combine(own, r1, l1, r2, l2)
+        right_pairs = [(c * 2 + k, (c + 1) % n_chip * 2 + k) for c in range(n_chip) for k in range(2)]
+        left_pairs = [(b, a) for a, b in right_pairs]
+        from_left = lax.ppermute(to_right, "ep", right_pairs)
+        from_right = lax.ppermute(to_left, "ep", left_pairs)
+        g_gate, g_up, g_down = weight_grads(xb, dz, h, da, db)
+        dx = combine(own, from_left, from_right)
         return dx, g_gate, g_down, g_up
 
     tok_spec = P(("dp", "ep"), None)

time: 56.9 us -> 59.1 us (1.039)
  Pallas kernels: 50.3 us -> 55 us
  starting transfers between devices: 5.5 us -> 3.31 us
    pallas_call x1, Pallas kernels: 32.7 us -> 38.5 us  [run_exchange(): pl.pallas_call(functools.partial(exchange_kernel, n_dev, cap), out_shape=...]
    ppermute x4 -> x2, starting transfers between devices: 5.5 us -> 3.31 us  [the longest x1 2.61 us: local_step(): from_right = lax.ppermute(to_left, 'ep', left_pairs)]
    pallas_call x2 -> x1, Pallas kernels: 16.8 us -> 15.7 us  [weight_grads(): pl.pallas_call(functools.partial(grads_kernel, in_blk, out_blk), out_shap...]
  transfers between devices with their start and end apart: 4 -> 2, of which waited for: 1 -> 0; matrix products, arithmetic and copies ran while one was open for 0% -> 0% of each run, Pallas kernels for 30% -> 27%
where the time goes in v3:
time: 59.1 us; the launch traced here: 58.9 us
  Pallas kernels  55 us (93%)
  starting transfers between devices  3.31 us (6%)
  between operations  0.67 us (1%)
    pallas_call x1, Pallas kernels, run_exchange(): pl.pallas_call(functools.partial(exchange_kernel, n_dev, cap), out_shape=...  38.5 us
    pallas_call x1, Pallas kernels, weight_grads(): pl.pallas_call(functools.partial(grads_kernel, in_blk, out_blk), out_shap...  15.7 us
    ppermute x1, starting transfers between devices, local_step(): from_right = lax.ppermute(to_left, 'ep', left_pairs)  2.61 us
  transfers between devices with their start and end apart: 2, of which 0 were waited for; matrix products, arithmetic and copies ran while one was open for 0% of the time, Pallas kernels for 27%

profile of v3, /device:TPU:112, one launch (start us, length us, event | category | flops | bytes accessed | tf_op | source)
XLA Modules:
  0.0 58.9 jit_solution(1513214476983486987)
XLA Ops:
  0.6 38.5 %exchange.1 = (bf16[5,192,1536]{2,1,0:T(8,128)(2,1)S(1)}, bf16[5,192,1536]{2,1,0:T(8,128)(2,1)S(1)}, bf16[5,192,512]{2,1,0:T(8,128)(2,1)S(1)}, bf16[5,192,512]{2...) custom-call(bf16[64,1536]{1,0:T(8,128)(2,1)} %x_hbm.1, ...), custom_call_target="tpu_custom_call" | custom-call | tf_op jit(solution)/shard_map/exchange/pallas_call | solution.py:369
  39.1 0.7 %collective-permute-start = (f32[64,1536]{1,0:T(8,128)S(1)}, f32[64,1536]{1,0:T(8,128)S(1)}, u32[]{:S(2)}, u32[]{:S(2)}) collective-permute-start(f32[64,1536]{1,0:T(8,128)S(1)} %get-tuple-element.16), channel_id=1, source_target_pairs={{0,2},{1,3},{2,4},{3,5},{4,6},{5,7},{6,0},{7,1},{8,10},{9,11},{10,... | collective-permute-start | bytes 1179656 | tf_op jit(solution)/shard_map/ppermute | solution.py:477
  39.9 2.6 %collective-permute-start.1 = (f32[64,1536]{1,0:T(8,128)S(1)}, f32[64,1536]{1,0:T(8,128)S(1)}, u32[]{:S(2)}, u32[]{:S(2)}) collective-permute-start(f32[64,1536]{1,0:T(8,128)S(1)} %get-tuple-element.17), channel_id=1, source_target_pairs={{2,0},{3,1},{4,2},{5,3},{6,4},{7,5},{0,6},{1,7},{10,8},{11,9},{12,... | collective-permute-start | bytes 1179656 | tf_op jit(solution)/shard_map/ppermute | solution.py:478
  42.5 15.7 %weight_grads.1 = (f32[5,1536,512]{2,1,0:T(8,128)}, f32[5,1536,512]{2,1,0:T(8,128)}, f32[5,512,1536]{2,1,0:T(8,128)}) custom-call(bf16[5,192,1536]{2,1,0:T(8,128)(2,1)S(1)} %get-tuple-element.18.x, bf16[5,192,1536]{2,1,0:T(8,128)(2,1)S(1)} %get-tuple-element.19.dz, bf16[5,192,512]{2,1,0:T(8,128)(2,1)S(1)} %get-tuple-element.20.h, ...), custom_call_target="tpu_custom_call" | custom-call | flops 4529848320 | bytes 47185920 | tf_op jit(solution)/shard_map/weight_grads/pallas_call | solution.py:436
  58.1 0.0 collective-permute-done.from_left
  58.1 0.0 collective-permute-done.1.from_right
  58.2 0.8 %combine.1 = bf16[64,1536]{1,0:T(8,128)(2,1)} custom-call(f32[64,1536]{1,0:T(8,128)S(1)} %get-tuple-element.15.own, f32[64,1536]{1,0:T(8,128)S(1)} %collective-permute-done.from_left, f32[64,1536]{1,0:T(8,128)S(1)} %collective-permute-done.1.from_right), custom_call_target="tpu_custom_call" | custom-call | tf_op jit(solution)/shard_map/combine/pallas_call | solution.py:455
Async XLA Ops:
  39.1 19.0 %collective-permute-start = (f32[64,1536]{1,0:T(8,128)S(1)}, f32[64,1536]{1,0:T(8,128)S(1)}, u32[]{:S(2)}, u32[]{:S(2)}) collective-permute-start(f32[64,1536]{1,0:T(8,128)S(1)} %get-tuple-element.16), channel_id=1, source_target_pairs={{0,2},{1,3},{2,4},{3,5},{4,6},{5,7},{6,0},{7,1},{8,10},{9,11},{10,... | collective-permute-start | bytes 1179656 | tf_op jit(solution)/shard_map/ppermute | solution.py:477
  39.9 18.3 %collective-permute-start.1 = (f32[64,1536]{1,0:T(8,128)S(1)}, f32[64,1536]{1,0:T(8,128)S(1)}, u32[]{:S(2)}, u32[]{:S(2)}) collective-permute-start(f32[64,1536]{1,0:T(8,128)S(1)} %get-tuple-element.17), channel_id=1, source_target_pairs={{2,0},{3,1},{4,2},{5,3},{6,4},{7,5},{0,6},{1,7},{10,8},{11,9},{12,... | collective-permute-start | bytes 1179656 | tf_op jit(solution)/shard_map/ppermute | solution.py:478

commit v4 on v2

--- a/solution.py
+++ b/solution.py
@@ -14,7 +14,8 @@
 DY_Q = 3
 DX_Q = 3
 KEY_STRIDE = 256
-N_COPIES = 36
+N_COPIES = 57
+N_GROUPS = 16
 OUT_TYPE = pltpu.VMEM
 
 
@@ -28,7 +29,7 @@
     xb, dz, hh, da, db, r1, l1, ra, lb, own,
     xg, dyg, ids, slots, gates_v, mt, w1, w3, w2, qq, uu, bb, dh, dxq,
     pm, pt, gm, part, sibr,
-    loc_sem, w_sem, send, recv,
+    loc_sem, w_sem, send_sem, recv_sem,
 ):
     n_exp = w1_hbm.shape[0]
     tok, d = x_hbm.shape
@@ -44,18 +45,19 @@
 
     counter = [0]
 
-    def remote(src, dst, dev):
-        i = counter[0]
+    groups = []
+
+    def describe(src, dst, dev, send_i, recv_i):
+        return pltpu.make_async_remote_copy(
+            src_ref=src, dst_ref=dst, send_sem=send_sem.at[send_i], recv_sem=recv_sem.at[recv_i],
+            device_id={"ep": dev}, device_id_type=pl.DeviceIdType.MESH)
+
+    def go(src, dst, dev, group):
+        if group not in groups:
+            groups.append(group)
+        copy = describe(src, dst, dev, groups.index(group), counter[0])
         counter[0] += 1
-        return pltpu.make_async_remote_copy(
-            src_ref=src, dst_ref=dst, send_sem=send.at[i], recv_sem=recv.at[i],
-            device_id={"ep": dev}, device_id_type=pl.DeviceIdType.MESH)
-
-    started = []
-
-    def go(copy):
         copy.start()
-        started.append(copy)
         return copy
 
     barrier = pltpu.get_barrier_semaphore()
@@ -71,9 +73,10 @@
     for c in loc:
         c.start()
     wcopies = {}
-    for k, (src, dst) in enumerate(((w1_hbm, w1), (w3_hbm, w3), (w2_hbm, w2))):
+    for k, (src, dst) in enumerate(((w1_hbm, w1), (w3_hbm, w3))):
         for e in range(n_exp):
             wcopies[k, e] = pltpu.make_async_copy(src.at[e], dst.at[e], w_sem.at[k * n_exp + e])
+    w2copy = pltpu.make_async_copy(w2_hbm, w2, w_sem.at[2 * n_exp])
 
     with jax.named_scope("head_keys"):
         for c in loc[:3]:
@@ -108,11 +111,11 @@
         pt[s] = jnp.transpose(ones).astype(BF16)
         gm[s] = jnp.sum(gmat, axis=1, keepdims=True)
 
-    def gather_x(s):
-        src = xg[s].reshape(2 * tok, d)
+    def gather_x(s, c):
+        src = xg[s, :, :, c].reshape(2 * tok, c.stop - c.start)
         rows = jnp.dot(pm[s, :used, :], src, preferred_element_type=F32).astype(BF16)
         for e in range(n_exp):
-            xb[e, s * rc_rows:(s + 1) * rc_rows, :] = rows[e * rc_rows:(e + 1) * rc_rows, :]
+            xb[e, s * rc_rows:(s + 1) * rc_rows, c] = rows[e * rc_rows:(e + 1) * rc_rows, :]
 
     def gather_dy(s, c):
         src = dyg[s, :, :, c].reshape(2 * tok, c.stop - c.start)
@@ -121,12 +124,19 @@
         for e in range(n_exp):
             dz[e, s * rc_rows:(s + 1) * rc_rows, c] = rows[e * rc_rows:(e + 1) * rc_rows, :]
 
-    def up(e):
+    hcol = [slice(0, d // 2), slice(d // 2, d)]
+
+    def up_first(e):
         wcopies[0, e].wait()
         wcopies[1, e].wait()
-        x = xb[e]
-        a16 = jnp.dot(x, w1[e], preferred_element_type=F32).astype(BF16)
-        b16 = jnp.dot(x, w3[e], preferred_element_type=F32).astype(BF16)
+        x = xb[e, :, hcol[0]]
+        qq[e] = jnp.dot(x, w1[e, hcol[0], :], preferred_element_type=F32)
+        uu[e] = jnp.dot(x, w3[e, hcol[0], :], preferred_element_type=F32)
+
+    def up_second(e):
+        x = xb[e, :, hcol[1]]
+        a16 = (qq[e] + jnp.dot(x, w1[e, hcol[1], :], preferred_element_type=F32)).astype(BF16)
+        b16 = (uu[e] + jnp.dot(x, w3[e, hcol[1], :], preferred_element_type=F32)).astype(BF16)
         a = a16.astype(F32)
         b = b16.astype(F32)
         sg = jax.nn.sigmoid(a)
@@ -141,111 +151,142 @@
     dcol = [slice(q * qd, (q + 1) * qd) for q in range(DY_Q)]
     full = slice(0, d)
 
-    def far_cols(q):
-        return pl.ds(q * qd, qd)
-
-    m_r = go(remote(mt.at[0, 0], mt.at[3, 0], right))
-    m_l = go(remote(mt.at[0, 0], mt.at[1, 0], left))
-    m_s = go(remote(mt.at[0, 0], mt.at[0, 1], sib))
+    def label(buf, kind):
+        return ("x" if buf is xg else "y") + kind
+
+    def send(buf, slot, rows, c, dev_slot, dev, kind):
+        cs = pl.ds(c.start, c.stop - c.start)
+        return go(buf.at[slot, 0, rows, cs], buf.at[dev_slot, 0, rows, cs], dev, label(buf, kind))
+
+    def forward(buf, slot, c):
+        cs = pl.ds(c.start, c.stop - c.start)
+        return go(buf.at[slot, 0, :, cs], buf.at[slot, 1, :, cs], sib, label(buf, "s"))
+
+    def to_right(buf, rows, c):
+        return send(buf, 0, rows, c, 3, right, "r")
+
+    def to_left(buf, rows, c):
+        return send(buf, 0, rows, c, 1, left, "l")
+
+    x, y = {}, {}
+
+    def near_pair(t, buf, c, k, first):
+        if first:
+            t["ar", k], t["bl", k] = to_right(buf, lo, c), to_left(buf, hi, c)
+        else:
+            t["br", k], t["al", k] = to_right(buf, hi, c), to_left(buf, lo, c)
+
+    def relay(t, buf, c, k):
+        t["ar", k].wait_recv()
+        t["arr", k] = send(buf, 3, lo, c, 2, right, "rr")
+        t["bl", k].wait_recv()
+        t["bll", k] = send(buf, 1, hi, c, 2, left, "ll")
+
+    def near_forward(t, buf, c, k):
+        t["br", k].wait_recv()
+        t["s3", k] = forward(buf, 3, c)
+        t["al", k].wait_recv()
+        t["s1", k] = forward(buf, 1, c)
+
+    def far_forward(t, buf, c, k):
+        t["arr", k].wait_recv()
+        t["bll", k].wait_recv()
+        t["s2", k] = forward(buf, 2, c)
+
+    m_r = go(mt.at[0, 0], mt.at[3, 0], right, "mr")
+    m_l = go(mt.at[0, 0], mt.at[1, 0], left, "ml")
+    m_s = go(mt.at[0, 0], mt.at[0, 1], sib, "ms")
     loc[3].wait()
-    xa_r = go(remote(xg.at[0, 0, lo], xg.at[3, 0, lo], right))
-    xb_l = go(remote(xg.at[0, 0, hi], xg.at[1, 0, hi], left))
-    xb_r = go(remote(xg.at[0, 0, hi], xg.at[3, 0, hi], right))
-    xa_l = go(remote(xg.at[0, 0, lo], xg.at[1, 0, lo], left))
-    x_s = go(remote(xg.at[0, 0], xg.at[0, 1], sib))
+    near_pair(x, xg, hcol[0], 0, True)
+    near_pair(x, xg, hcol[0], 0, False)
+    near_pair(x, xg, hcol[1], 1, True)
+    x["s0", 0] = forward(xg, 0, full)
     loc[4].wait()
-    y_s = go(remote(dyg.at[0, 0], dyg.at[0, 1], sib))
+    y["s0", 0] = forward(dyg, 0, full)
     for e in range(n_exp):
         wcopies[0, e].start()
         wcopies[1, e].start()
-    for e in range(n_exp):
-        wcopies[2, e].start()
+    w2copy.start()
     with jax.named_scope("own_rows"):
         m_s.wait_recv()
         build(0)
         m_r.wait_recv()
-        m_rr = go(remote(mt.at[3, 0], mt.at[2, 0], right))
-        m_s3 = go(remote(mt.at[3, 0], mt.at[3, 1], sib))
+        m_rr = go(mt.at[3, 0], mt.at[2, 0], right, "mr")
+        m_s3 = go(mt.at[3, 0], mt.at[3, 1], sib, "ms")
         m_l.wait_recv()
-        m_s1 = go(remote(mt.at[1, 0], mt.at[1, 1], sib))
-        x_s.wait_recv()
-        gather_x(0)
-    with jax.named_scope("x_relay"):
-        xa_r.wait_recv()
-        xa_rr = go(remote(xg.at[3, 0, lo], xg.at[2, 0, lo], right))
-        xb_l.wait_recv()
-        xb_ll = go(remote(xg.at[1, 0, hi], xg.at[2, 0, hi], left))
-        ya_r = go(remote(dyg.at[0, 0, lo], dyg.at[3, 0, lo], right))
-        yb_l = go(remote(dyg.at[0, 0, hi], dyg.at[1, 0, hi], left))
-        yb_r = go(remote(dyg.at[0, 0, hi], dyg.at[3, 0, hi], right))
-        ya_l = go(remote(dyg.at[0, 0, lo], dyg.at[1, 0, lo], left))
-    with jax.named_scope("build31"):
+        m_s1 = go(mt.at[1, 0], mt.at[1, 1], sib, "ms")
+        x["s0", 0].wait_recv()
+        gather_x(0, full)
+    with jax.named_scope("x_relay0"):
+        relay(x, xg, hcol[0], 0)
+        near_pair(x, xg, hcol[1], 1, False)
+    with jax.named_scope("build3"):
         m_s3.wait_recv()
         build(3)
+    with jax.named_scope("x_near_fwd0"):
+        near_forward(x, xg, hcol[0], 0)
+    with jax.named_scope("x_relay1"):
+        relay(x, xg, hcol[1], 1)
+        for k in (0, 1):
+            near_pair(y, dyg, dcol[k], k, True)
+            near_pair(y, dyg, dcol[k], k, False)
+        m_rr.wait_recv()
+        m_s2 = go(mt.at[2, 0], mt.at[2, 1], sib, "ms")
+    with jax.named_scope("build1"):
         m_s1.wait_recv()
         build(1)
-    with jax.named_scope("x_near"):
-        xb_r.wait_recv()
-        x_s3 = go(remote(xg.at[3, 0], xg.at[3, 1], sib))
-        xa_l.wait_recv()
-        x_s1 = go(remote(xg.at[1, 0], xg.at[1, 1], sib))
-        m_rr.wait_recv()
-        m_s2 = go(remote(mt.at[2, 0], mt.at[2, 1], sib))
-        y_s.wait_recv()
-        gather_dy(0, full)
-        x_s3.wait_recv()
-        gather_x(3)
-        x_s1.wait_recv()
-        gather_x(1)
-    with jax.named_scope("x_far"):
+        x["s3", 0].wait_recv()
+        gather_x(3, hcol[0])
+        x["s1", 0].wait_recv()
+        gather_x(1, hcol[0])
+    with jax.named_scope("x_far_fwd0"):
+        far_forward(x, xg, hcol[0], 0)
+    with jax.named_scope("build2"):
         m_s2.wait_recv()
         build(2)
-        xa_rr.wait_recv()
-        xb_ll.wait_recv()
-        x_s2 = go(remote(xg.at[2, 0], xg.at[2, 1], sib))
-        x_s2.wait_recv()
-        gather_x(2)
-    with jax.named_scope("up0"):
-        up(0)
-    with jax.named_scope("y_relay"):
-        ya_r.wait_recv()
-        yb_l.wait_recv()
-        yfar = []
-        for q in range(DY_Q):
-            c = far_cols(q)
-            yfar.append((go(remote(dyg.at[3, 0, lo, c], dyg.at[2, 0, lo, c], right)),
-                         go(remote(dyg.at[1, 0, hi, c], dyg.at[2, 0, hi, c], left))))
-    with jax.named_scope("up12"):
-        up(1)
-        up(2)
-    with jax.named_scope("y_near_fwd"):
-        yb_r.wait_recv()
-        y_s3 = go(remote(dyg.at[3, 0], dyg.at[3, 1], sib))
-        ya_l.wait_recv()
-        y_s1 = go(remote(dyg.at[1, 0], dyg.at[1, 1], sib))
-    with jax.named_scope("up34"):
-        for e in range(3, n_exp):
-            up(e)
-
-    y_s2 = []
-
-    def y_far_fwd(q):
-        c = far_cols(q)
-        for copy in yfar[q]:
-            copy.wait_recv()
-        y_s2.append(go(remote(dyg.at[2, 0, :, c], dyg.at[2, 1, :, c], sib)))
-
-    with jax.named_scope("y_near"):
-        y_far_fwd(0)
-        y_s3.wait_recv()
-        gather_dy(3, full)
-        y_s1.wait_recv()
-        gather_dy(1, full)
+    with jax.named_scope("x_near_fwd1"):
+        near_forward(x, xg, hcol[1], 1)
+    with jax.named_scope("x_far0"):
+        x["s2", 0].wait_recv()
+        gather_x(2, hcol[0])
+    with jax.named_scope("up_first01"):
+        up_first(0)
+        up_first(1)
+    with jax.named_scope("x_far_fwd1"):
+        far_forward(x, xg, hcol[1], 1)
+    with jax.named_scope("up_first234"):
+        for e in range(2, n_exp):
+            up_first(e)
+    with jax.named_scope("y_relay0"):
+        relay(y, dyg, dcol[0], 0)
+        near_pair(y, dyg, dcol[2], 2, True)
+        near_pair(y, dyg, dcol[2], 2, False)
+        near_forward(y, dyg, dcol[0], 0)
+    with jax.named_scope("x_rest"):
+        for slot in (3, 1, 2):
+            x["s%d" % slot, 1].wait_recv()
+            gather_x(slot, hcol[1])
+    with jax.named_scope("up_second01"):
+        up_second(0)
+        up_second(1)
+    with jax.named_scope("y_relay1"):
+        relay(y, dyg, dcol[1], 1)
+        near_forward(y, dyg, dcol[1], 1)
+    with jax.named_scope("up_second23"):
+        up_second(2)
+        up_second(3)
+    with jax.named_scope("y_far_fwd0"):
+        far_forward(y, dyg, dcol[0], 0)
+    with jax.named_scope("up_second4"):
+        for e in range(4, n_exp):
+            up_second(e)
+    with jax.named_scope("y_relay2"):
+        relay(y, dyg, dcol[2], 2)
+        y["s0", 0].wait_recv()
+        gather_dy(0, full)
 
     def down(e, q):
         c = dcol[q]
-        if q == 0:
-            wcopies[2, e].wait()
         val = lax.dot_general(dz[e, :, c], w2[e, :, c], NT, preferred_element_type=F32)
         if q > 0:
             val = val + dh[e]
@@ -255,15 +296,26 @@
             da[e] = (val * bb[e].astype(F32) * qq[e]).astype(BF16)
             db[e] = (val * uu[e]).astype(BF16)
 
+    w2copy.wait()
     for q in range(DY_Q):
+        with jax.named_scope(f"y_near{q}"):
+            for slot in (3, 1):
+                y["s%d" % slot, q].wait_recv()
+                gather_dy(slot, dcol[q])
+        with jax.named_scope(f"y_fwd{q}"):
+            if q == 0:
+                near_forward(y, dyg, dcol[2], 2)
+            if q == 1:
+                far_forward(y, dyg, dcol[2], 2)
         with jax.named_scope(f"y_far{q}"):
-            if q + 1 < DY_Q:
-                y_far_fwd(q + 1)
-            y_s2[q].wait_recv()
+            y["s2", q].wait_recv()
             gather_dy(2, dcol[q])
         with jax.named_scope(f"down{q}"):
             for e in range(n_exp):
                 down(e, q)
+        if q == 0:
+            with jax.named_scope("y_far_fwd1"):
+                far_forward(y, dyg, dcol[1], 1)
 
     qx = d // DX_Q
     sib_copies = []
@@ -277,7 +329,7 @@
         for s in range(n_chip):
             rows = dxq[:, s * rc_rows:(s + 1) * rc_rows, :].reshape(used, qx)
             part[q, s] = jnp.dot(pt[s, :, :used], rows, preferred_element_type=F32).reshape(2, tok, qx)
-        sib_copies.append(go(remote(part.at[q, :, 1], sibr.at[q], sib)))
+        sib_copies.append(go(part.at[q, :, 1], sibr.at[q], sib, "p%d" % q))
 
     def finish(q):
         c = slice(q * qx, (q + 1) * qx)
@@ -305,9 +357,15 @@
         finish(DX_Q - 1)
 
     with jax.named_scope("send_wait"):
-        for c in started:
-            c.wait_send()
-    assert counter[0] == N_COPIES
+        whole = {"mr": mt.at[0], "ml": mt.at[0, 0], "ms": mt.at[:, 0]}
+        for name, buf in (("x", xg), ("y", dyg)):
+            whole.update({name + "r": buf.at[0, 0], name + "l": buf.at[0, 0], name + "s": buf.at[:, 0],
+                          name + "rr": buf.at[0, 0, lo], name + "ll": buf.at[0, 0, hi]})
+        for q in range(DX_Q):
+            whole["p%d" % q] = part.at[q, :, 1]
+        for i, group in enumerate(groups):
+            describe(whole[group], whole[group], sib, i, 0).wait_send()
+    assert (counter[0], len(groups)) == (N_COPIES, N_GROUPS)
 
 
 def run_exchange(x, dy, ids, slots, gates, w1, w3, w2, n_dev, cap):
@@ -347,8 +405,8 @@
         pltpu.VMEM((DX_Q, n_chip, 2, tok, qx), F32),
         pltpu.VMEM((DX_Q, n_chip, tok, qx), F32),
         pltpu.SemaphoreType.DMA((5,)),
-        pltpu.SemaphoreType.DMA((3 * n_exp,)),
-        pltpu.SemaphoreType.DMA((N_COPIES,)),
+        pltpu.SemaphoreType.DMA((2 * n_exp + 1,)),
+        pltpu.SemaphoreType.DMA((N_GROUPS,)),
         pltpu.SemaphoreType.DMA((N_COPIES,)),
     ]
     return pl.pallas_call(

time: 56.9 us -> 59.1 us (1.039)
  Pallas kernels: 50.3 us -> 52.2 us
    pallas_call x1, Pallas kernels: 32.7 us -> 34.6 us  [run_exchange(): pl.pallas_call(functools.partial(exchange_kernel, n_dev, cap), out_shape=...]
  transfers between devices with their start and end apart: 4 -> 4, of which waited for: 1 -> 1; matrix products, arithmetic and copies ran while one was open for 0% -> 0% of each run, Pallas kernels for 30% -> 29%
where the time goes in v4:
time: 59.1 us; the launch traced here: 59 us
  Pallas kernels  52.2 us (88%)
  starting transfers between devices  5.5 us (9%)
  between operations  0.69 us (1%)
    pallas_call x1, Pallas kernels, run_exchange(): pl.pallas_call(functools.partial(exchange_kernel, n_dev, cap), out_shape=...  34.6 us
    pallas_call x1, Pallas kernels, grad_in(): pl.pallas_call(functools.partial(grad_in_kernel, blk), out_shape=(out, ou...  10.8 us
    pallas_call x1, Pallas kernels, grad_out(): pl.pallas_call(functools.partial(grad_out_kernel, blk), out_shape=out, in...  6.01 us
    ppermute x1, starting transfers between devices, local_step(): l1 = lax.ppermute(l1, 'ep', to_left)  2.74 us
    ppermute x1, starting transfers between devices, local_step(): l2 = lax.ppermute(lb + l1[half:], 'ep', to_left)  1.62 us
  transfers between devices with their start and end apart: 4, of which 1 were waited for; matrix products, arithmetic and copies ran while one was open for 0% of the time, Pallas kernels for 29%

profile of v4, /device:TPU:112, one launch (start us, length us, event | category | flops | bytes accessed | tf_op | source)
XLA Modules:
  0.0 59.0 jit_solution(2094789260634071378)
XLA Ops:
  0.6 34.6 %exchange.1 = (bf16[5,192,1536]{2,1,0:T(8,128)(2,1)S(1)}, bf16[5,192,1536]{2,1,0:T(8,128)(2,1)S(1)}, bf16[5,192,512]{2,1,0:T(8,128)(2,1)S(1)}, bf16[5,192,512]{2...) custom-call(bf16[64,1536]{1,0:T(8,128)(2,1)} %x_hbm.1, ...), custom_call_target="tpu_custom_call" | custom-call | tf_op jit(solution)/shard_map/exchange/pallas_call | solution.py:412
  35.3 0.6 collective-permute-start
  35.8 2.7 %collective-permute-start.1 = (f32[64,1536]{1,0:T(8,128)S(1)}, f32[64,1536]{1,0:T(8,128)S(1)}, u32[]{:S(2)}, u32[]{:S(2)}) collective-permute-start(f32[64,1536]{1,0:T(8,128)S(1)} %get-tuple-element.27), channel_id=1, source_target_pairs={{2,0},{3,1},{4,2},{5,3},{6,4},{7,5},{0,6},{1,7},{10,8},{11,9},{12,... | collective-permute-start | bytes 1179656 | tf_op jit(solution)/shard_map/ppermute | solution.py:545
  38.6 10.8 %grad_in.1 = (f32[5,1536,512]{2,1,0:T(8,128)}, f32[5,1536,512]{2,1,0:T(8,128)}) custom-call(bf16[5,192,1536]{2,1,0:T(8,128)(2,1)S(1)} %get-tuple-element.21.x, bf16[5,192,512]{2,1,0:T(8,128)(2,1)S(1)} %get-tuple-element.22.da, bf16[5,192,512]{2,1,0:T(8,128)(2,1)S(1)} %get-tuple-element.23.db), custom_call_target="tpu_custom_call" | custom-call | flops 3019898880 | bytes 31457280 | tf_op jit(solution)/shard_map/grad_in/pallas_call | solution.py:459
  49.4 0.0 collective-permute-done.r1
  49.4 0.0 collective-permute-done.1.l1
  49.5 1.6 %collective-permute-start.3 = (f32[32,1536]{1,0:T(8,128)S(1)}, f32[32,1536]{1,0:T(8,128)S(1)}, u32[]{:S(2)}, u32[]{:S(2)}) collective-permute-start(f32[32,1536]{1,0:T(8,128)S(1)} %slice_add_fusion), channel_id=1, source_target_pairs={{2,0},{3,1},{4,2},{5,3},{6,4},{7,5},{0,6},{1,7},{10,8},{11,9},{12,... | collective-permute-start | bytes 589832 | tf_op jit(solution)/shard_map/ppermute | solution.py:549
  51.1 0.6 collective-permute-start.2
  51.7 6.0 %grad_out.1 = f32[5,512,1536]{2,1,0:T(8,128)} custom-call(bf16[5,192,512]{2,1,0:T(8,128)(2,1)S(1)} %get-tuple-element.33.h, bf16[5,192,1536]{2,1,0:T(8,128)(2,1)S(1)} %get-tuple-element.34.dz), custom_call_target="tpu_custom_call" | custom-call | flops 1509949440 | bytes 15728640 | tf_op jit(solution)/shard_map/grad_out/pallas_call | solution.py:502
  57.7 0.0 collective-permute-done.3.l2
  57.7 0.5 collective-permute-done.2.r2
  58.2 0.7 %combine.1 = bf16[64,1536]{1,0:T(8,128)(2,1)} custom-call(f32[64,1536]{1,0:T(8,128)S(1)} %get-tuple-element.20.own, f32[64,1536]{1,0:T(8,128)S(1)} %collective-permute-done.r1, f32[64,1536]{1,0:T(8,128)S(1)} %collective-permute-done.1.l1, f32[32,1536]{1,0:T(8,128)S(1)} %collective-permute-done.2.r2, f32[32,1536]{1,0:T(8,128)S(1)} %collective-permute-done.3.l2), custom_call_target="tpu_custom_call" | custom-call | tf_op jit(solution)/shard_map/combine/pallas_call | solution.py:521
  (2 shorter events, 0.1 us)
Async XLA Ops:
  35.3 14.2 %collective-permute-start = (f32[64,1536]{1,0:T(8,128)S(1)}, f32[64,1536]{1,0:T(8,128)S(1)}, u32[]{:S(2)}, u32[]{:S(2)}) collective-permute-start(f32[64,1536]{1,0:T(8,128)S(1)} %get-tuple-element.26), channel_id=1, source_target_pairs={{0,2},{1,3},{2,4},{3,5},{4,6},{5,7},{6,0},{7,1},{8,10},{9,11},{10,... | collective-permute-start | bytes 1179656 | tf_op jit(solution)/shard_map/ppermute | solution.py:544
  35.8 13.6 %collective-permute-start.1 = (f32[64,1536]{1,0:T(8,128)S(1)}, f32[64,1536]{1,0:T(8,128)S(1)}, u32[]{:S(2)}, u32[]{:S(2)}) collective-permute-start(f32[64,1536]{1,0:T(8,128)S(1)} %get-tuple-element.27), channel_id=1, source_target_pairs={{2,0},{3,1},{4,2},{5,3},{6,4},{7,5},{0,6},{1,7},{10,8},{11,9},{12,... | collective-permute-start | bytes 1179656 | tf_op jit(solution)/shard_map/ppermute | solution.py:545
  49.5 8.2 %collective-permute-start.3 = (f32[32,1536]{1,0:T(8,128)S(1)}, f32[32,1536]{1,0:T(8,128)S(1)}, u32[]{:S(2)}, u32[]{:S(2)}) collective-permute-start(f32[32,1536]{1,0:T(8,128)S(1)} %slice_add_fusion), channel_id=1, source_target_pairs={{2,0},{3,1},{4,2},{5,3},{6,4},{7,5},{0,6},{1,7},{10,8},{11,9},{12,... | collective-permute-start | bytes 589832 | tf_op jit(solution)/shard_map/ppermute | solution.py:549
  51.1 7.1 %collective-permute-start.2 = (f32[32,1536]{1,0:T(8,128)S(1)}, f32[32,1536]{1,0:T(8,128)S(1)}, u32[]{:S(2)}, u32[]{:S(2)}) collective-permute-start(f32[32,1536]{1,0:T(8,128)S(1)} %slice_add_fusion.1), channel_id=1, source_target_pairs={{0,2},{1,3},{2,4},{3,5},{4,6},{5,7},{6,0},{7,1},{8,10},{9,11},{10,... | collective-permute-start | bytes 589832 | tf_op jit(solution)/shard_map/ppermute | solution.py:548

commit v5 on v2

--- a/solution.py
+++ b/solution.py
@@ -15,6 +15,7 @@
 DX_Q = 3
 KEY_STRIDE = 256
 N_COPIES = 36
+N_GROUPS = 16
 OUT_TYPE = pltpu.VMEM
 
 
@@ -28,7 +29,7 @@
     xb, dz, hh, da, db, r1, l1, ra, lb, own,
     xg, dyg, ids, slots, gates_v, mt, w1, w3, w2, qq, uu, bb, dh, dxq,
     pm, pt, gm, part, sibr,
-    loc_sem, w_sem, send, recv,
+    loc_sem, w_sem, send_sem, recv_sem,
 ):
     n_exp = w1_hbm.shape[0]
     tok, d = x_hbm.shape
@@ -44,18 +45,19 @@
 
     counter = [0]
 
-    def remote(src, dst, dev):
-        i = counter[0]
+    groups = []
+
+    def describe(src, dst, dev, send_i, recv_i):
+        return pltpu.make_async_remote_copy(
+            src_ref=src, dst_ref=dst, send_sem=send_sem.at[send_i], recv_sem=recv_sem.at[recv_i],
+            device_id={"ep": dev}, device_id_type=pl.DeviceIdType.MESH)
+
+    def go(src, dst, dev, group):
+        if group not in groups:
+            groups.append(group)
+        copy = describe(src, dst, dev, groups.index(group), counter[0])
         counter[0] += 1
-        return pltpu.make_async_remote_copy(
-            src_ref=src, dst_ref=dst, send_sem=send.at[i], recv_sem=recv.at[i],
-            device_id={"ep": dev}, device_id_type=pl.DeviceIdType.MESH)
-
-    started = []
-
-    def go(copy):
         copy.start()
-        started.append(copy)
         return copy
 
     barrier = pltpu.get_barrier_semaphore()
@@ -71,9 +73,10 @@
     for c in loc:
         c.start()
     wcopies = {}
-    for k, (src, dst) in enumerate(((w1_hbm, w1), (w3_hbm, w3), (w2_hbm, w2))):
+    for k, (src, dst) in enumerate(((w1_hbm, w1), (w3_hbm, w3))):
         for e in range(n_exp):
             wcopies[k, e] = pltpu.make_async_copy(src.at[e], dst.at[e], w_sem.at[k * n_exp + e])
+    w2copy = pltpu.make_async_copy(w2_hbm, w2, w_sem.at[2 * n_exp])
 
     with jax.named_scope("head_keys"):
         for c in loc[:3]:
@@ -144,41 +147,40 @@
     def far_cols(q):
         return pl.ds(q * qd, qd)
 
-    m_r = go(remote(mt.at[0, 0], mt.at[3, 0], right))
-    m_l = go(remote(mt.at[0, 0], mt.at[1, 0], left))
-    m_s = go(remote(mt.at[0, 0], mt.at[0, 1], sib))
+    m_r = go(mt.at[0, 0], mt.at[3, 0], right, "mr")
+    m_l = go(mt.at[0, 0], mt.at[1, 0], left, "ml")
+    m_s = go(mt.at[0, 0], mt.at[0, 1], sib, "ms")
     loc[3].wait()
-    xa_r = go(remote(xg.at[0, 0, lo], xg.at[3, 0, lo], right))
-    xb_l = go(remote(xg.at[0, 0, hi], xg.at[1, 0, hi], left))
-    xb_r = go(remote(xg.at[0, 0, hi], xg.at[3, 0, hi], right))
-    xa_l = go(remote(xg.at[0, 0, lo], xg.at[1, 0, lo], left))
-    x_s = go(remote(xg.at[0, 0], xg.at[0, 1], sib))
+    xa_r = go(xg.at[0, 0, lo], xg.at[3, 0, lo], right, "xr")
+    xb_l = go(xg.at[0, 0, hi], xg.at[1, 0, hi], left, "xl")
+    xb_r = go(xg.at[0, 0, hi], xg.at[3, 0, hi], right, "xr")
+    xa_l = go(xg.at[0, 0, lo], xg.at[1, 0, lo], left, "xl")
+    x_s = go(xg.at[0, 0], xg.at[0, 1], sib, "xs")
     loc[4].wait()
-    y_s = go(remote(dyg.at[0, 0], dyg.at[0, 1], sib))
+    y_s = go(dyg.at[0, 0], dyg.at[0, 1], sib, "ys")
     for e in range(n_exp):
         wcopies[0, e].start()
         wcopies[1, e].start()
-    for e in range(n_exp):
-        wcopies[2, e].start()
+    w2copy.start()
     with jax.named_scope("own_rows"):
         m_s.wait_recv()
         build(0)
         m_r.wait_recv()
-        m_rr = go(remote(mt.at[3, 0], mt.at[2, 0], right))
-        m_s3 = go(remote(mt.at[3, 0], mt.at[3, 1], sib))
+        m_rr = go(mt.at[3, 0], mt.at[2, 0], right, "mr")
+        m_s3 = go(mt.at[3, 0], mt.at[3, 1], sib, "ms")
         m_l.wait_recv()
-        m_s1 = go(remote(mt.at[1, 0], mt.at[1, 1], sib))
+        m_s1 = go(mt.at[1, 0], mt.at[1, 1], sib, "ms")
         x_s.wait_recv()
         gather_x(0)
     with jax.named_scope("x_relay"):
         xa_r.wait_recv()
-        xa_rr = go(remote(xg.at[3, 0, lo], xg.at[2, 0, lo], right))
+        xa_rr = go(xg.at[3, 0, lo], xg.at[2, 0, lo], right, "xrr")
         xb_l.wait_recv()
-        xb_ll = go(remote(xg.at[1, 0, hi], xg.at[2, 0, hi], left))
-        ya_r = go(remote(dyg.at[0, 0, lo], dyg.at[3, 0, lo], right))
-        yb_l = go(remote(dyg.at[0, 0, hi], dyg.at[1, 0, hi], left))
-        yb_r = go(remote(dyg.at[0, 0, hi], dyg.at[3, 0, hi], right))
-        ya_l = go(remote(dyg.at[0, 0, lo], dyg.at[1, 0, lo], left))
+        xb_ll = go(xg.at[1, 0, hi], xg.at[2, 0, hi], left, "xll")
+        ya_r = go(dyg.at[0, 0, lo], dyg.at[3, 0, lo], right, "yr")
+        yb_l = go(dyg.at[0, 0, hi], dyg.at[1, 0, hi], left, "yl")
+        yb_r = go(dyg.at[0, 0, hi], dyg.at[3, 0, hi], right, "yr")
+        ya_l = go(dyg.at[0, 0, lo], dyg.at[1, 0, lo], left, "yl")
     with jax.named_scope("build31"):
         m_s3.wait_recv()
         build(3)
@@ -186,11 +188,11 @@
         build(1)
     with jax.named_scope("x_near"):
         xb_r.wait_recv()
-        x_s3 = go(remote(xg.at[3, 0], xg.at[3, 1], sib))
+        x_s3 = go(xg.at[3, 0], xg.at[3, 1], sib, "xs")
         xa_l.wait_recv()
-        x_s1 = go(remote(xg.at[1, 0], xg.at[1, 1], sib))
+        x_s1 = go(xg.at[1, 0], xg.at[1, 1], sib, "xs")
         m_rr.wait_recv()
-        m_s2 = go(remote(mt.at[2, 0], mt.at[2, 1], sib))
+        m_s2 = go(mt.at[2, 0], mt.at[2, 1], sib, "ms")
         y_s.wait_recv()
         gather_dy(0, full)
         x_s3.wait_recv()
@@ -202,7 +204,7 @@
         build(2)
         xa_rr.wait_recv()
         xb_ll.wait_recv()
-        x_s2 = go(remote(xg.at[2, 0], xg.at[2, 1], sib))
+        x_s2 = go(xg.at[2, 0], xg.at[2, 1], sib, "xs")
         x_s2.wait_recv()
         gather_x(2)
     with jax.named_scope("up0"):
@@ -213,16 +215,16 @@
         yfar = []
         for q in range(DY_Q):
             c = far_cols(q)
-            yfar.append((go(remote(dyg.at[3, 0, lo, c], dyg.at[2, 0, lo, c], right)),
-                         go(remote(dyg.at[1, 0, hi, c], dyg.at[2, 0, hi, c], left))))
+            yfar.append((go(dyg.at[3, 0, lo, c], dyg.at[2, 0, lo, c], right, "yrr"),
+                         go(dyg.at[1, 0, hi, c], dyg.at[2, 0, hi, c], left, "yll")))
     with jax.named_scope("up12"):
         up(1)
         up(2)
     with jax.named_scope("y_near_fwd"):
         yb_r.wait_recv()
-        y_s3 = go(remote(dyg.at[3, 0], dyg.at[3, 1], sib))
+        y_s3 = go(dyg.at[3, 0], dyg.at[3, 1], sib, "ys")
         ya_l.wait_recv()
-        y_s1 = go(remote(dyg.at[1, 0], dyg.at[1, 1], sib))
+        y_s1 = go(dyg.at[1, 0], dyg.at[1, 1], sib, "ys")
     with jax.named_scope("up34"):
         for e in range(3, n_exp):
             up(e)
@@ -233,7 +235,7 @@
         c = far_cols(q)
         for copy in yfar[q]:
             copy.wait_recv()
-        y_s2.append(go(remote(dyg.at[2, 0, :, c], dyg.at[2, 1, :, c], sib)))
+        y_s2.append(go(dyg.at[2, 0, :, c], dyg.at[2, 1, :, c], sib, "ys"))
 
     with jax.named_scope("y_near"):
         y_far_fwd(0)
@@ -244,8 +246,6 @@
 
     def down(e, q):
         c = dcol[q]
-        if q == 0:
-            wcopies[2, e].wait()
         val = lax.dot_general(dz[e, :, c], w2[e, :, c], NT, preferred_element_type=F32)
         if q > 0:
             val = val + dh[e]
@@ -255,6 +255,7 @@
             da[e] = (val * bb[e].astype(F32) * qq[e]).astype(BF16)
             db[e] = (val * uu[e]).astype(BF16)
 
+    w2copy.wait()
     for q in range(DY_Q):
         with jax.named_scope(f"y_far{q}"):
             if q + 1 < DY_Q:
@@ -271,13 +272,13 @@
     def dx_block(q):
         c = slice(q * qx, (q + 1) * qx)
         for e in range(n_exp):
-            v = lax.dot_general(da[e], w1[e, c, :], NT, preferred_element_type=F32)
-            v = v + lax.dot_general(db[e], w3[e, c, :], NT, preferred_element_type=F32)
-            dxq[e] = v.astype(BF16)
+            v = lax.dot_general(w1[e, c, :], da[e], NT, preferred_element_type=F32)
+            v = v + lax.dot_general(w3[e, c, :], db[e], NT, preferred_element_type=F32)
+            dxq[e] = jnp.transpose(v).astype(BF16)
         for s in range(n_chip):
             rows = dxq[:, s * rc_rows:(s + 1) * rc_rows, :].reshape(used, qx)
             part[q, s] = jnp.dot(pt[s, :, :used], rows, preferred_element_type=F32).reshape(2, tok, qx)
-        sib_copies.append(go(remote(part.at[q, :, 1], sibr.at[q], sib)))
+        sib_copies.append(go(part.at[q, :, 1], sibr.at[q], sib, "p%d" % q))
 
     def finish(q):
         c = slice(q * qx, (q + 1) * qx)
@@ -305,9 +306,15 @@
         finish(DX_Q - 1)
 
     with jax.named_scope("send_wait"):
-        for c in started:
-            c.wait_send()
-    assert counter[0] == N_COPIES
+        whole = {"mr": mt.at[0], "ml": mt.at[0, 0], "ms": mt.at[:, 0]}
+        for name, buf in (("x", xg), ("y", dyg)):
+            whole.update({name + "r": buf.at[0, 0], name + "l": buf.at[0, 0], name + "s": buf.at[:, 0],
+                          name + "rr": buf.at[0, 0, lo], name + "ll": buf.at[0, 0, hi]})
+        for q in range(DX_Q):
+            whole["p%d" % q] = part.at[q, :, 1]
+        for i, group in enumerate(groups):
+            describe(whole[group], whole[group], sib, i, 0).wait_send()
+    assert (counter[0], len(groups)) == (N_COPIES, N_GROUPS)
 
 
 def run_exchange(x, dy, ids, slots, gates, w1, w3, w2, n_dev, cap):
@@ -347,8 +354,8 @@
         pltpu.VMEM((DX_Q, n_chip, 2, tok, qx), F32),
         pltpu.VMEM((DX_Q, n_chip, tok, qx), F32),
         pltpu.SemaphoreType.DMA((5,)),
-        pltpu.SemaphoreType.DMA((3 * n_exp,)),
-        pltpu.SemaphoreType.DMA((N_COPIES,)),
+        pltpu.SemaphoreType.DMA((2 * n_exp + 1,)),
+        pltpu.SemaphoreType.DMA((N_GROUPS,)),
         pltpu.SemaphoreType.DMA((N_COPIES,)),
     ]
     return pl.pallas_call(

time: 56.9 us -> 56.5 us (level)
  no operation moved by 1% of the time
where the time goes in v5:
time: 56.5 us; the launch traced here: 56.3 us
  Pallas kernels  49.9 us (88%)
  starting transfers between devices  5.5 us (10%)
  between operations  0.69 us (1%)
    pallas_call x1, Pallas kernels, run_exchange(): pl.pallas_call(functools.partial(exchange_kernel, n_dev, cap), out_shape=...  32.3 us
    pallas_call x1, Pallas kernels, grad_in(): pl.pallas_call(functools.partial(grad_in_kernel, blk), out_shape=(out, ou...  10.8 us
    pallas_call x1, Pallas kernels, grad_out(): pl.pallas_call(functools.partial(grad_out_kernel, blk), out_shape=out, in...  6.01 us
    ppermute x1, starting transfers between devices, local_step(): l1 = lax.ppermute(l1, 'ep', to_left)  2.81 us
    ppermute x1, starting transfers between devices, local_step(): l2 = lax.ppermute(lb + l1[half:], 'ep', to_left)  1.46 us
  transfers between devices with their start and end apart: 4, of which 1 were waited for; matrix products, arithmetic and copies ran while one was open for 0% of the time, Pallas kernels for 30%

profile of v5, /device:TPU:112, one launch (start us, length us, event | category | flops | bytes accessed | tf_op | source)
XLA Modules:
  0.0 56.3 jit_solution(15104461799455800330)
XLA Ops:
  0.6 32.3 %exchange.1 = (bf16[5,192,1536]{2,1,0:T(8,128)(2,1)S(1)}, bf16[5,192,1536]{2,1,0:T(8,128)(2,1)S(1)}, bf16[5,192,512]{2,1,0:T(8,128)(2,1)S(1)}, bf16[5,192,512]{2...) custom-call(bf16[64,1536]{1,0:T(8,128)(2,1)} %x_hbm.1, ...), custom_call_target="tpu_custom_call" | custom-call | tf_op jit(solution)/shard_map/exchange/pallas_call | solution.py:361
  32.9 0.5 collective-permute-start
  33.4 2.8 %collective-permute-start.1 = (f32[64,1536]{1,0:T(8,128)S(1)}, f32[64,1536]{1,0:T(8,128)S(1)}, u32[]{:S(2)}, u32[]{:S(2)}) collective-permute-start(f32[64,1536]{1,0:T(8,128)S(1)} %get-tuple-element.27), channel_id=1, source_target_pairs={{2,0},{3,1},{4,2},{5,3},{6,4},{7,5},{0,6},{1,7},{10,8},{11,9},{12,... | collective-permute-start | bytes 1179656 | tf_op jit(solution)/shard_map/ppermute | solution.py:494
  36.3 10.8 %grad_in.1 = (f32[5,1536,512]{2,1,0:T(8,128)}, f32[5,1536,512]{2,1,0:T(8,128)}) custom-call(bf16[5,192,1536]{2,1,0:T(8,128)(2,1)S(1)} %get-tuple-element.21.x, bf16[5,192,512]{2,1,0:T(8,128)(2,1)S(1)} %get-tuple-element.22.da, bf16[5,192,512]{2,1,0:T(8,128)(2,1)S(1)} %get-tuple-element.23.db), custom_call_target="tpu_custom_call" | custom-call | flops 3019898880 | bytes 31457280 | tf_op jit(solution)/shard_map/grad_in/pallas_call | solution.py:408
  47.1 0.0 collective-permute-done.r1
  47.1 0.0 collective-permute-done.1.l1
  47.1 1.5 %collective-permute-start.3 = (f32[32,1536]{1,0:T(8,128)S(1)}, f32[32,1536]{1,0:T(8,128)S(1)}, u32[]{:S(2)}, u32[]{:S(2)}) collective-permute-start(f32[32,1536]{1,0:T(8,128)S(1)} %slice_add_fusion), channel_id=1, source_target_pairs={{2,0},{3,1},{4,2},{5,3},{6,4},{7,5},{0,6},{1,7},{10,8},{11,9},{12,... | collective-permute-start | bytes 589832 | tf_op jit(solution)/shard_map/ppermute | solution.py:498
  48.6 0.7 %collective-permute-start.2 = (f32[32,1536]{1,0:T(8,128)S(1)}, f32[32,1536]{1,0:T(8,128)S(1)}, u32[]{:S(2)}, u32[]{:S(2)}) collective-permute-start(f32[32,1536]{1,0:T(8,128)S(1)} %slice_add_fusion.1), channel_id=1, source_target_pairs={{0,2},{1,3},{2,4},{3,5},{4,6},{5,7},{6,0},{7,1},{8,10},{9,11},{10,... | collective-permute-start | bytes 589832 | tf_op jit(solution)/shard_map/ppermute | solution.py:497
  49.4 6.0 %grad_out.1 = f32[5,512,1536]{2,1,0:T(8,128)} custom-call(bf16[5,192,512]{2,1,0:T(8,128)(2,1)S(1)} %get-tuple-element.33.h, bf16[5,192,1536]{2,1,0:T(8,128)(2,1)S(1)} %get-tuple-element.34.dz), custom_call_target="tpu_custom_call" | custom-call | flops 1509949440 | bytes 15728640 | tf_op jit(solution)/shard_map/grad_out/pallas_call | solution.py:451
  55.4 0.0 collective-permute-done.3.l2
  55.4 0.2 collective-permute-done.2.r2
  55.6 0.7 %combine.1 = bf16[64,1536]{1,0:T(8,128)(2,1)} custom-call(f32[64,1536]{1,0:T(8,128)S(1)} %get-tuple-element.20.own, f32[64,1536]{1,0:T(8,128)S(1)} %collective-permute-done.r1, f32[64,1536]{1,0:T(8,128)S(1)} %collective-permute-done.1.l1, f32[32,1536]{1,0:T(8,128)S(1)} %collective-permute-done.2.r2, f32[32,1536]{1,0:T(8,128)S(1)} %collective-permute-done.3.l2), custom_call_target="tpu_custom_call" | custom-call | tf_op jit(solution)/shard_map/combine/pallas_call | solution.py:470
  (2 shorter events, 0.1 us)
Async XLA Ops:
  32.9 14.2 %collective-permute-start = (f32[64,1536]{1,0:T(8,128)S(1)}, f32[64,1536]{1,0:T(8,128)S(1)}, u32[]{:S(2)}, u32[]{:S(2)}) collective-permute-start(f32[64,1536]{1,0:T(8,128)S(1)} %get-tuple-element.26), channel_id=1, source_target_pairs={{0,2},{1,3},{2,4},{3,5},{4,6},{5,7},{6,0},{7,1},{8,10},{9,11},{10,... | collective-permute-start | bytes 1179656 | tf_op jit(solution)/shard_map/ppermute | solution.py:493
  33.4 13.7 %collective-permute-start.1 = (f32[64,1536]{1,0:T(8,128)S(1)}, f32[64,1536]{1,0:T(8,128)S(1)}, u32[]{:S(2)}, u32[]{:S(2)}) collective-permute-start(f32[64,1536]{1,0:T(8,128)S(1)} %get-tuple-element.27), channel_id=1, source_target_pairs={{2,0},{3,1},{4,2},{5,3},{6,4},{7,5},{0,6},{1,7},{10,8},{11,9},{12,... | collective-permute-start | bytes 1179656 | tf_op jit(solution)/shard_map/ppermute | solution.py:494
  47.1 8.2 %collective-permute-start.3 = (f32[32,1536]{1,0:T(8,128)S(1)}, f32[32,1536]{1,0:T(8,128)S(1)}, u32[]{:S(2)}, u32[]{:S(2)}) collective-permute-start(f32[32,1536]{1,0:T(8,128)S(1)} %slice_add_fusion), channel_id=1, source_target_pairs={{2,0},{3,1},{4,2},{5,3},{6,4},{7,5},{0,6},{1,7},{10,8},{11,9},{12,... | collective-permute-start | bytes 589832 | tf_op jit(solution)/shard_map/ppermute | solution.py:498
  48.6 7.0 %collective-permute-start.2 = (f32[32,1536]{1,0:T(8,128)S(1)}, f32[32,1536]{1,0:T(8,128)S(1)}, u32[]{:S(2)}, u32[]{:S(2)}) collective-permute-start(f32[32,1536]{1,0:T(8,128)S(1)} %slice_add_fusion.1), channel_id=1, source_target_pairs={{0,2},{1,3},{2,4},{3,5},{4,6},{5,7},{6,0},{7,1},{8,10},{9,11},{10,... | collective-permute-start | bytes 589832 | tf_op jit(solution)/shard_map/ppermute | solution.py:497
